TPU v7x, 128 devices: a 2x2x16 block of a 8x8x16 slice. The times are simulated.
128 devices in a mesh: grp: 4 (over y, x), band: 32 (over z, core).
Axes of the slice: x: 2, y: 2, z: 16, core: 2. Of those that a mesh axis runs over, the one named last changes fastest.
The devices are a block of a 8x8x16 slice.
Arguments:
- source: bfloat16 [1048576, 640], P(('grp', 'band')), parts along dimension 0, may hold values from -96 to 96
- tiles: bfloat16 [8192, 128, 128], P('band'), may hold values from 0 to 0.001953125
- tile_slot: int32 [8192], P('band'), may hold values from 0 to 63, as said below
- tile_dst: int32 [8192], P('band'), may hold values from 0 to 31
- send_index: int32 [32, 64], P('band'), may hold values from 0 to 63
- send_count: int32 [32, 32], P('band'), may hold values from 1 to 2, as said below
- polar_tiles: bfloat16 [2048, 128, 128], P('band'), may hold values from 0 to 0.00024414062
- polar_src: int32 [2048], P('band'), may hold values from 0 to 63
- polar_dst: int32 [2048], P('band'), may hold values from 0 to 31
Outputs:
- model_field: bfloat16 [524288, 640], P(('grp', 'band')), parts along dimension 0
- polar_cap: bfloat16 [16384, 640], P(('grp', 'band')), parts along dimension 0
There are 4 independent parts, one for each index of `grp`. A program takes and returns all parts, laid end to end along the dimension named above; an argument that names none is the same for every part. Nothing has to cross between parts.
Inputs may be any that keep to these rules, and one draw needn't show every extreme that they name: `send_count`: entry [s, o] counts the used slots of band s for owner o; every row has an entry 2, and some owner has 2 from every band. `tile_slot`: tile t names slot s * 2 + j of owner t // 256 with j below send_count[s, t // 256]; every used slot is named by some tile of its owner.
All inputs are finite; a program needn't handle non-finite values.
Results may differ from a plain program's by a relative error of at most 0.001.
Values may be sent and summed in bfloat16 or wider, within the bound.
No kernel may reach another device: no remote copies, remote signals or barrier semaphores. Data moves between devices by JAX's collectives and lax.ppermute only.
A program may use at most 192 MiB of HBM per device.

v0:
```python
import jax
import jax.numpy as jnp
from jax import lax
from jax.sharding import Mesh
from jax.sharding import PartitionSpec as P

PB_DEV = 1
TB_DEV = 32
BAND = ("band_0", "band_1")
GRP_BAND = ("grp", "band_0", "band_1")


def split_up(array, dim, devices):
    before, after = (array.shape[:dim], array.shape[dim + 1 :])
    return jnp.moveaxis(array.reshape(*before, devices, -1, *after), dim, 0)


def joined_along(pieces, dim):
    shape = list(pieces.shape[1:])
    shape[dim] *= pieces.shape[0]
    return jnp.moveaxis(pieces, 0, dim).reshape(shape)


def turned_blocks(pieces, axes, order):
    inside = pieces.shape[1:]
    out = pieces.reshape(*(lax.axis_size(a) for a in axes), *inside)
    for k in order:
        out = lax.all_to_all(out, axes[k], k, k, tiled=True)
    return out.reshape(-1, *inside)


def core_and_chips(array, groups, order, split_dim, concat_dim):
    devices = lax.axis_size(groups[0]) * lax.axis_size(groups[1])
    pieces = split_up(array, split_dim, devices)
    return joined_along(turned_blocks(pieces, groups, order), concat_dim)


def on_device(
    source, tiles, tile_slot, tile_dst, send_index, send_count, polar_tiles, polar_src, polar_dst
):
    owners = lax.axis_size(BAND)
    width = tiles.shape[1]
    feats = source.shape[1]
    per_owner = send_index.shape[1] // owners
    blocks = source.reshape(-1, width, feats)
    polar_inputs = blocks[polar_src]
    polar_terms = jnp.einsum(
        "tps,tsf->tpf", polar_tiles, polar_inputs, preferred_element_type=jnp.float32
    )
    cap_part = (
        jnp.zeros((PB_DEV * owners, width, feats), jnp.float32).at[polar_dst].add(polar_terms)
    )
    usable = lax.broadcasted_iota(jnp.int32, (owners, per_owner), 1) < send_count[0][:, None]
    outgoing = blocks[send_index[0]]
    outgoing = jnp.where(usable.reshape(-1)[:, None, None], outgoing, jnp.zeros((), jnp.bfloat16))
    received = lax.all_to_all(
        outgoing.reshape(owners, per_owner, width, feats),
        BAND,
        split_axis=0,
        concat_axis=0,
        tiled=True,
    )
    arrived = received.reshape(owners * per_owner, width, feats)
    group = 32
    turns = tiles.shape[0] // group

    def accumulate(total, items):
        weights, slots, places = items
        inputs = arrived[slots]
        products = jnp.einsum("tps,tsf->tpf", weights, inputs, preferred_element_type=jnp.float32)
        return (total.at[places].add(products), None)

    field, _ = lax.scan(
        accumulate,
        jnp.zeros((TB_DEV, width, feats), jnp.float32),
        (
            tiles.reshape(turns, group, width, width),
            tile_slot.reshape(turns, group),
            tile_dst.reshape(turns, group),
        ),
    )
    rounded = field.astype(jnp.bfloat16).reshape(TB_DEV // owners, owners, width, feats)
    placed = core_and_chips(rounded, ("band_0", "band_1"), (1, 0), 1, 0)
    model_field = placed.reshape(TB_DEV * width, feats)
    own_cap = lax.psum_scatter(cap_part, BAND, scatter_dimension=0, tiled=True)
    polar_cap = own_cap.reshape(PB_DEV * width, feats).astype(jnp.bfloat16)
    return (model_field, polar_cap)


def solution(mesh):
    torus = Mesh(mesh.devices.reshape(mesh.shape["grp"], 16, 2), ("grp", "band_0", "band_1"))
    in_specs = (
        P(GRP_BAND, None),
        P(BAND, None, None),
        P(BAND),
        P(BAND),
        P(BAND, None),
        P(BAND, None),
        P(BAND, None, None),
        P(BAND),
        P(BAND),
    )
    out_specs = (P(GRP_BAND, None), P(GRP_BAND, None))
    return jax.shard_map(
        on_device, mesh=torus, in_specs=in_specs, out_specs=out_specs, check_vma=False
    )
```

profile of v0, /device:TPU:69, one launch (start us, length us, event | category | flops | bytes accessed | tf_op | source)
XLA Modules:
  0.0 1107.3 jit_solution(2450610683623144165)
XLA Ops:
  8.7 10.7 gather_fusion.1
  19.5 10.0 broadcast_select_fusion
  29.5 18.7 %all-to-all-start = ((bf16[32,2,128,640]{3,2,1,0:T(8,128)(2,1)}), bf16[32,2,128,640]{3,2,1,0:T(8,128)(2,1)}, u32[]{:S(2)}, u32[]{:S(2)}) async-start(bf16[32,2,128,640]{3,2,1,0:T(8,128)(2,1)} %broadcast_select_fusion), calls=%async_computation | async-start | bytes 20971520 | tf_op jit(solution)/shard_map/all_to_all | solution.py:56
  48.4 10.7 gather_fusion.2
  59.1 11.0 convolution_bitcast_fusion
  70.2 22.7 %copy.20 = f32[64,128,640]{2,1,0:T(8,128)} copy(f32[64,128,640]{1,2,0:T(8,128)} %convolution_bitcast_fusion) | data formatting | bytes 41943040 | tf_op jit(solution)/shard_map/tps,tsf->tpf/dot_general | solution.py:47
  98.0 42.2 %scatter_fusion.1 = f32[32,128,640]{2,1,0:T(8,128)} fusion(f32[32,128,640]{2,1,0:T(8,128)} %broadcast.71.clone.1, s32[64]{0:T(128)S(1)} %compare_select_fusion.3, f32[64,128,640]{2,1,0:T(8,128)} %copy.20), kind=kCustom, calls=%fused_computation.4 | custom fusion | flops 5242880 | bytes 62914816 | tf_op jit(solution)/shard_map/scatter-add | solution.py:51
  141.1 400.1 %all-to-all-done = bf16[32,2,128,640]{3,2,1,0:T(8,128)(2,1)} async-done(((bf16[32,2,128,640]{3,2,1,0:T(8,128)(2,1)}), bf16[32,2,128,640]{3,2,1,0:T(8,128)(2,1)}, u32[]{:S(2)}, u32[]{:S(2)}) %all-to-all-start) | async-done | bytes 10485792 | tf_op jit(solution)/shard_map/all_to_all | solution.py:56
  546.2 298.5 %while.10 = (s32[]{:T(128)}, f32[32,128,640]{2,1,0:T(8,128)}, s32[8,32]{1,0:T(8,128)S(1)}, bf16[8,32,128,128]{3,2,1,0:T(8,128)(2,1)}, s32[8,32]{1,0:T(8,128)S(1)}, /*index=5*/bf16[64,128,640]{2,1,0:T(8,128)(2,1)}, s32[]{:T(128)}) while((s32[]{:T(128)}, f32[32,128,640]{2,1,0:T(8,128)}, s32[8,32]{1,0:T(8,128)S(1)}, ...), condition=%wide.region_2.3_spmd, body=%wide.region_0.2_spmd.sunk | while | flops 673711296 | bytes 58725840 | solution.py:73
  546.2 7.7 gather_fusion
  553.9 8.4 fusion.19
  562.3 21.4 %scatter_fusion = f32[32,128,640]{2,1,0:T(8,128)} fusion(f32[32,128,640]{2,1,0:T(8,128)} %get-tuple-element.98, s32[32]{0:T(128)S(1)} %get-tuple-element.88, f32[32,128,640]{2,1,0:T(8,128)} %fusion.19), kind=kCustom, calls=%fused_computation.3.clone.1 | custom fusion | flops 2621440 | bytes 31457408 | tf_op jit(solution)/shard_map/while/body/eval_jaxpr/scatter-add | solution.py:71
  591.2 8.3 fusion.19
  599.5 21.4 %scatter_fusion = f32[32,128,640]{2,1,0:T(8,128)} fusion(f32[32,128,640]{2,1,0:T(8,128)} %get-tuple-element.98, s32[32]{0:T(128)S(1)} %get-tuple-element.88, f32[32,128,640]{2,1,0:T(8,128)} %fusion.19), kind=kCustom, calls=%fused_computation.3.clone.1 | custom fusion | flops 2621440 | bytes 31457408 | tf_op jit(solution)/shard_map/while/body/eval_jaxpr/scatter-add | solution.py:71
  620.9 7.5 gather_fusion
  628.5 8.3 fusion.19
  636.8 21.2 %scatter_fusion = f32[32,128,640]{2,1,0:T(8,128)} fusion(f32[32,128,640]{2,1,0:T(8,128)} %get-tuple-element.98, s32[32]{0:T(128)S(1)} %get-tuple-element.88, f32[32,128,640]{2,1,0:T(8,128)} %fusion.19), kind=kCustom, calls=%fused_computation.3.clone.1 | custom fusion | flops 2621440 | bytes 31457408 | tf_op jit(solution)/shard_map/while/body/eval_jaxpr/scatter-add | solution.py:71
  658.0 7.5 gather_fusion
  665.5 8.3 fusion.19
  673.8 21.6 %scatter_fusion = f32[32,128,640]{2,1,0:T(8,128)} fusion(f32[32,128,640]{2,1,0:T(8,128)} %get-tuple-element.98, s32[32]{0:T(128)S(1)} %get-tuple-element.88, f32[32,128,640]{2,1,0:T(8,128)} %fusion.19), kind=kCustom, calls=%fused_computation.3.clone.1 | custom fusion | flops 2621440 | bytes 31457408 | tf_op jit(solution)/shard_map/while/body/eval_jaxpr/scatter-add | solution.py:71
  703.0 8.3 fusion.19
  711.3 21.4 %scatter_fusion = f32[32,128,640]{2,1,0:T(8,128)} fusion(f32[32,128,640]{2,1,0:T(8,128)} %get-tuple-element.98, s32[32]{0:T(128)S(1)} %get-tuple-element.88, f32[32,128,640]{2,1,0:T(8,128)} %fusion.19), kind=kCustom, calls=%fused_computation.3.clone.1 | custom fusion | flops 2621440 | bytes 31457408 | tf_op jit(solution)/shard_map/while/body/eval_jaxpr/scatter-add | solution.py:71
  732.7 7.5 gather_fusion
  740.2 8.3 fusion.19
  748.5 21.4 %scatter_fusion = f32[32,128,640]{2,1,0:T(8,128)} fusion(f32[32,128,640]{2,1,0:T(8,128)} %get-tuple-element.98, s32[32]{0:T(128)S(1)} %get-tuple-element.88, f32[32,128,640]{2,1,0:T(8,128)} %fusion.19), kind=kCustom, calls=%fused_computation.3.clone.1 | custom fusion | flops 2621440 | bytes 31457408 | tf_op jit(solution)/shard_map/while/body/eval_jaxpr/scatter-add | solution.py:71
  770.0 7.5 gather_fusion
  777.5 8.3 fusion.19
  785.8 21.5 %scatter_fusion = f32[32,128,640]{2,1,0:T(8,128)} fusion(f32[32,128,640]{2,1,0:T(8,128)} %get-tuple-element.98, s32[32]{0:T(128)S(1)} %get-tuple-element.88, f32[32,128,640]{2,1,0:T(8,128)} %fusion.19), kind=kCustom, calls=%fused_computation.3.clone.1 | custom fusion | flops 2621440 | bytes 31457408 | tf_op jit(solution)/shard_map/while/body/eval_jaxpr/scatter-add | solution.py:71
  814.9 8.3 fusion.19
  823.2 21.6 %scatter_fusion = f32[32,128,640]{2,1,0:T(8,128)} fusion(f32[32,128,640]{2,1,0:T(8,128)} %get-tuple-element.98, s32[32]{0:T(128)S(1)} %get-tuple-element.88, f32[32,128,640]{2,1,0:T(8,128)} %fusion.19), kind=kCustom, calls=%fused_computation.3.clone.1 | custom fusion | flops 2621440 | bytes 31457408 | tf_op jit(solution)/shard_map/while/body/eval_jaxpr/scatter-add | solution.py:71
  850.3 8.4 all_to_all.15
  868.2 226.9 %all-to-all-done.2 = bf16[16,2,1,1,128,640]{5,4,1,3,2,0:T(8,128)(2,1)} async-done(((bf16[16,2,1,1,128,640]{5,4,1,3,2,0:T(8,128)(2,1)}), bf16[16,2,1,1,128,640]{5,4,1,3,2,0:T(8,128)(2,1)}, u32[]{:S(2)}, u32[]{:S(2)}) %all-to-all-start.2) | async-done | bytes 5242912 | tf_op jit(solution)/shard_map/all_to_all | solution.py:28
  (50 shorter events, 55.9 us)
Async XLA Ops:
  7.2 52.0 %copy-start = (bf16[64,128,128]{2,1,0:T(8,128)(2,1)S(1)}, bf16[64,128,128]{2,1,0:T(8,128)(2,1)}, u32[]{:S(2)}) copy-start(bf16[64,128,128]{2,1,0:T(8,128)(2,1)} %param.17) | copy-start | bytes 6291460
  29.5 18.9 %copy-start.4 = (s32[64]{0:T(128)S(1)}, s32[64]{0:T(128)}, u32[]{:S(2)}) copy-start(s32[64]{0:T(128)} %param.18) | copy-start | bytes 772
  29.5 511.7 %all-to-all-start = ((bf16[32,2,128,640]{3,2,1,0:T(8,128)(2,1)}), bf16[32,2,128,640]{3,2,1,0:T(8,128)(2,1)}, u32[]{:S(2)}, u32[]{:S(2)}) async-start(bf16[32,2,128,640]{3,2,1,0:T(8,128)(2,1)} %broadcast_select_fusion), calls=%async_computation | async-start | bytes 20971520 | tf_op jit(solution)/shard_map/all_to_all | solution.py:56
  48.1 818.5 %reduce-scatter.2.cloned.1.call-start = ((), (), s32[]{:S(2)}) async-start(), calls=%async_computation.4 | async-start | bytes 10813440 | tf_op jit(solution)/shard_map/reduce_scatter | solution.py:85
  70.2 22.7 %copy-start.5 = (s32[64]{0:T(128)S(1)}, s32[64]{0:T(128)}, u32[]{:S(2)}) copy-start(s32[64]{0:T(128)} %param.19) | copy-start | bytes 772
  140.2 0.7 copy-start.2
  140.2 0.8 copy-start.3
  858.7 241.8 %copy-start.1 = (bf16[64,128,128]{2,1,0:T(8,128)(2,1)S(1)}, bf16[64,128,128]{2,1,0:T(8,128)(2,1)}, u32[]{:S(2)}) copy-start(bf16[64,128,128]{2,1,0:T(8,128)(2,1)} %param.17) | copy-start | bytes 6291460
  861.5 233.7 %all-to-all-start.2 = ((bf16[16,2,1,1,128,640]{5,4,1,3,2,0:T(8,128)(2,1)}), bf16[16,2,1,1,128,640]{5,4,1,3,2,0:T(8,128)(2,1)}, u32[]{:S(2)}, u32[]{:S(2)}) async-start(bf16[16,2,1,1,128,640]{5,4,1,3,2,0:T(8,128)(2,1)} %copy.18), calls=%async_computation.2 | async-start | bytes 10485760 | tf_op jit(solution)/shard_map/all_to_all | solution.py:28
Sparse Core Ops, SparseCore 0:
  140.4 429.2 reduce-scatter.1
where the time goes:
time: 1110 us
  waiting for transfers between devices  627 us (56%)
  other arithmetic  232 us (21%)
  local copies, waits for them, and re-layouts  124 us (11%)
  matrix products  77.6 us (7%)
  starting transfers between devices  24 us (2%)
  between operations  14.1 us (1%)
    all_to_all x1, waiting for transfers between devices, on_device(): lax.all_to_all(outgoing.reshape(owners, per_owner, width, feats), BAND, s...  400 us
    all_to_all x1, waiting for transfers between devices, turned_blocks(): out = lax.all_to_all(out, axes[k], k, k, tiled=True)  227 us
    scatter-add x8, other arithmetic, accumulate(): return (total.at[places].add(products), None)  172 us
    dot_general x8, matrix products, accumulate(): jnp.einsum('tps,tsf->tpf', weights, inputs, preferred_element_type=jnp.fl...  66.5 us
    gather x8, local copies, waits for them, and re-layouts, accumulate(): inputs = arrived[slots]  60.3 us
    scatter-add x1, other arithmetic, on_device(): jnp.zeros((PB_DEV * owners, width, feats), jnp.float32).at[polar_dst]  42.2 us
    dot_general x1, local copies, waits for them, and re-layouts, on_device(): jnp.einsum('tps,tsf->tpf', polar_tiles, polar_inputs, preferred_element_t...  22.7 us
  transfers between devices with their start and end apart: 3, of which 2 were waited for; matrix products, arithmetic and copies ran while one was open for 37% of the time, Pallas kernels for 0%

commit v1 on v0

v1 whole, which is shorter than its diff:
```python
import functools

import jax
import jax.numpy as jnp
import numpy as np
from jax import lax
from jax.experimental import pallas as pl
from jax.experimental.pallas import tpu as pltpu
from jax.sharding import PartitionSpec as P


GRP_BAND = ("grp", "band")
CORES = 2
FIRST_PACK = 7
PHASES = (20, 30)
FIRST_SENT = 8
LAST_PLACED = 8
ANY = pl.BlockSpec(memory_space=pl.ANY)
SMEM = pl.BlockSpec(memory_space=pltpu.SMEM)
VMEM = pl.BlockSpec(memory_space=pltpu.VMEM)


def params(mib):
    return pltpu.CompilerParams(vmem_limit_bytes=mib * 2**20)


def cost(flops, moved):
    return pl.CostEstimate(flops=flops, bytes_accessed=moved, transcendentals=0)


def near_to_far(owners):
    chips = owners // CORES
    shifts = [(d, c) for d in range(chips) for c in range(CORES)]
    return sorted(shifts, key=lambda s: (min(s[0], chips - s[0]), s[1], s[0]))


def pairs(owners, shift):
    chips = owners // CORES
    return [
        (i, (i // CORES + shift[0]) % chips * CORES + (i % CORES + shift[1]) % CORES)
        for i in range(owners)
    ]


def moved(owners, me, hop, core):
    chips = owners // CORES
    return lax.rem(me // CORES + hop + chips, chips) * CORES + lax.rem(
        lax.rem(me, CORES) + core, CORES
    )


def pack_kernel(shifts, owners, me_ref, index_ref, count_ref, source_ref, *refs):
    outs, (held, blank, in_sems, out_sems) = refs[: len(shifts)], refs[len(shifts) :]
    per_owner = held.shape[1]
    targets = [moved(owners, me_ref[0], *s) for s in shifts]
    every = [(p, j) for p in range(len(shifts)) for j in range(per_owner)]

    def fetch(p, j):
        block = source_ref.at[index_ref[0, targets[p] * per_owner + j]]
        return pltpu.make_async_copy(block, held.at[p, j], in_sems.at[p, j])

    def put(p, j, block):
        return pltpu.make_async_copy(block, outs[p].at[j], out_sems.at[p, j])

    for p, j in every:
        fetch(p, j).start()
    blank[...] = jnp.zeros_like(blank)
    for p, j in every:
        fetch(p, j).wait()
        used = j < count_ref[0, targets[p]]

        @pl.when(used)
        def _():
            put(p, j, held.at[p, j]).start()

        @pl.when(jnp.logical_not(used))
        def _():
            put(p, j, blank).start()

    for p, j in every:
        put(p, j, held.at[p, j]).wait()


def pack(shifts, owners, me, blocks, index, count):
    inside = blocks.shape[1:]
    per_owner = index.shape[1] // owners
    shape = jax.ShapeDtypeStruct((per_owner, *inside), blocks.dtype)
    size = len(shifts) * per_owner * inside[0] * inside[1] * 2
    return pl.pallas_call(
        functools.partial(pack_kernel, shifts, owners),
        out_shape=[shape] * len(shifts),
        in_specs=[SMEM, SMEM, SMEM, ANY],
        out_specs=[ANY] * len(shifts),
        scratch_shapes=[
            pltpu.VMEM((len(shifts), per_owner, *inside), blocks.dtype),
            pltpu.VMEM(inside, blocks.dtype),
            pltpu.SemaphoreType.DMA((len(shifts), per_owner)),
            pltpu.SemaphoreType.DMA((len(shifts), per_owner)),
        ],
        compiler_params=params(58),
        cost_estimate=cost(0, 2 * size),
        name="pack",
    )(me, index, count, blocks)


def sums_kernel(
    n_inputs, start, bounds_ref, order_ref, slot_ref, place_ref, tiles_ref, *refs
):
    inputs, refs = refs[:n_inputs], refs[n_inputs:]
    if start is None:
        before = None
    else:
        before, refs = refs[0], refs[1:]
    outs, (held, weights, total, in_sems, tile_sems, sum_sem) = refs[:-6], refs[-6:]
    each = inputs[0].shape[0]
    depth = weights.shape[0]
    low, high = bounds_ref[0], bounds_ref[1]

    def fetch(k):
        return pltpu.make_async_copy(inputs[k], held.at[pl.ds(k * each, each)], in_sems.at[k])

    def fetch_tile(i):
        at = lax.rem(i, depth)
        return pltpu.make_async_copy(tiles_ref.at[order_ref[i]], weights.at[at], tile_sems.at[at])

    if before is None:
        for k in range(n_inputs):
            fetch(k).start()
    else:
        for k in range(n_inputs):
            held[pl.ds(k * each, each)] = inputs[k][...]
        sums = pltpu.make_async_copy(before.at[pl.ds(start, total.shape[0])], total, sum_sem)
        sums.start()

    @pl.loop(low, jnp.minimum(low + depth, high))
    def _(i):
        fetch_tile(i).start()

    if before is None:

        @pl.loop(0, total.shape[0])
        def _(b):
            total[b] = jnp.zeros(total.shape[1:], total.dtype)

        for k in range(n_inputs):
            fetch(k).wait()

    else:
        sums.wait()

    @pl.loop(low, high)
    def _(i):
        fetch_tile(i).wait()
        t = order_ref[i]
        place = place_ref[t]
        total[place] += jnp.dot(
            weights[lax.rem(i, depth)], held[slot_ref[t]], preferred_element_type=jnp.float32
        )

        @pl.when(i + depth < high)
        def _():
            fetch_tile(i + depth).start()

    if len(outs) == 1:

        @pl.loop(0, total.shape[0])
        def _(b):
            outs[0][b] = total[b].astype(outs[0].dtype)

    else:
        for b, out in enumerate(outs):
            out[...] = total[b].astype(out.dtype)


def sums(inputs, tiles, bounds, order, slots, places, blocks, start, before, split, dtype):
    each, width, feats = inputs[0].shape
    depth = 16
    if split:
        shape = [jax.ShapeDtypeStruct((width, feats), dtype)] * blocks
    else:
        shape = [jax.ShapeDtypeStruct((blocks, width, feats), dtype)]
    work = tiles.shape[0] * blocks * len(inputs) // 1024
    return pl.pallas_call(
        functools.partial(sums_kernel, len(inputs), None if before is None else start),
        out_shape=shape,
        in_specs=[SMEM] * 4
        + [ANY]
        + ([ANY] * len(inputs) if before is None else [VMEM] * len(inputs) + [ANY]),
        out_specs=[VMEM] * len(shape),
        scratch_shapes=[
            pltpu.VMEM((len(inputs) * each, width, feats), inputs[0].dtype),
            pltpu.VMEM((depth, width, width), tiles.dtype),
            pltpu.VMEM((blocks, width, feats), jnp.float32),
            pltpu.SemaphoreType.DMA((len(inputs),)),
            pltpu.SemaphoreType.DMA((depth,)),
            pltpu.SemaphoreType.DMA,
        ],
        compiler_params=params(58 if before is None else 40),
        cost_estimate=cost(2 * work * width * width * feats, blocks * width * feats * 6),
    )(bounds, order, slots, places, tiles, *inputs, *([] if before is None else [before]))


def place_kernel(shifts, owners, aliased, me_ref, *refs):
    blocks, (out_ref, sems) = refs[aliased : aliased + len(shifts)], refs[-2:]

    def put(p):
        at = moved(owners, me_ref[0], -shifts[p][0], shifts[p][1])
        return pltpu.make_async_copy(blocks[p], out_ref.at[at], sems.at[p])

    for p in range(len(shifts)):
        put(p).start()
    for p in range(len(shifts)):
        put(p).wait()


def place(shifts, owners, me, blocks, out):
    inside = blocks[0].shape
    given = [] if out is None else [out]
    return pl.pallas_call(
        functools.partial(place_kernel, shifts, owners, len(given)),
        out_shape=jax.ShapeDtypeStruct((owners, *inside), blocks[0].dtype),
        in_specs=[SMEM] + [ANY] * len(given) + [VMEM] * len(blocks),
        out_specs=ANY,
        scratch_shapes=[pltpu.SemaphoreType.DMA((len(shifts),))],
        input_output_aliases={1: 0} if given else {},
        compiler_params=params(12),
        cost_estimate=cost(0, 4 * len(blocks) * inside[0] * inside[1]),
        name="place",
    )(me, *given, *blocks)


def looked_up(table, at):
    hit = at[:, None] == lax.broadcasted_iota(jnp.int32, (1, len(table)), 1)
    return jnp.sum(jnp.where(hit, jnp.asarray(table, jnp.int32)[None, :], 0), axis=1)


def apart(owners, here, there):
    chips = owners // CORES
    hop = (there // CORES - here // CORES + chips) % chips
    return hop * CORES + (there % CORES - here % CORES + CORES) % CORES


def grouped(key, groups):
    n = key.shape[0]
    rows = lax.broadcasted_iota(jnp.int32, (n, n), 0)
    cols = lax.broadcasted_iota(jnp.int32, (n, n), 1)
    ahead = (key[None, :] < key[:, None]) | ((key[None, :] == key[:, None]) & (cols < rows))
    rank = jnp.sum(ahead.astype(jnp.int32), axis=1)
    order = jnp.sum(jnp.where(rank[None, :] == rows, cols, 0), axis=1)
    ends = [jnp.zeros((), jnp.int32)] + [
        jnp.sum((key <= g).astype(jnp.int32)) for g in range(groups)
    ]
    return order, [jnp.stack(ends[g : g + 2]) for g in range(groups)]


def polar_kernel(slot_ref, place_ref, tiles_ref, source_ref, out_ref, held, sem):
    copy = pltpu.make_async_copy(source_ref, held, sem)
    copy.start()

    @pl.loop(0, out_ref.shape[0])
    def _(b):
        out_ref[b] = jnp.zeros(out_ref.shape[1:], out_ref.dtype)

    copy.wait()

    @pl.loop(0, tiles_ref.shape[0])
    def _(t):
        out_ref[place_ref[t]] += jnp.dot(
            tiles_ref[t], held[slot_ref[t]], preferred_element_type=jnp.float32
        )


def polar_sums(tiles, slots, places, source, blocks):
    width, feats = source.shape[1:]
    return pl.pallas_call(
        polar_kernel,
        out_shape=jax.ShapeDtypeStruct((blocks, width, feats), jnp.float32),
        in_specs=[SMEM, SMEM, VMEM, ANY],
        out_specs=VMEM,
        scratch_shapes=[pltpu.VMEM(source.shape, source.dtype), pltpu.SemaphoreType.DMA],
        compiler_params=params(58),
        cost_estimate=cost(2 * tiles.size * feats, source.size * 2 + blocks * width * feats * 4),
        name="polar",
    )(slots, places, tiles, source)


def regridded(
    source, tiles, tile_slot, tile_dst, send_index, send_count, polar_tiles, polar_src, polar_dst
):
    owners = lax.axis_size("band")
    width, feats = tiles.shape[1], source.shape[1]
    per_owner = send_index.shape[1] // owners
    blocks = source.reshape(-1, width, feats)
    here = lax.axis_index("band").astype(jnp.int32)
    me = here.reshape(1)

    def send(array, shift):
        return array if shift == (0, 0) else lax.ppermute(array, "band", pairs(owners, shift))

    near = near_to_far(owners)
    own, first, rest = near[:1], near[1:FIRST_PACK], near[FIRST_PACK:]
    arrived = {}
    for part in (first, rest + own):
        packed = pack(part, owners, me, blocks, send_index, send_count)
        for shift, block in zip(part, packed):
            arrived[shift] = send(block, shift)

    cap_part = polar_sums(polar_tiles, polar_src, polar_dst, blocks, owners)
    own_cap = lax.psum_scatter(cap_part, "band", scatter_dimension=0, tiled=True)

    far = near[::-1]
    rows = [s[0] * CORES + s[1] for s in near]
    near_at, far_at = np.argsort(rows), np.argsort(rows[::-1])
    cuts = (0, *PHASES, owners)
    shift_at = looked_up(near_at, apart(owners, tile_slot // per_owner, here))
    places = looked_up(far_at, apart(owners, here, tile_dst))
    phase = sum((shift_at >= c).astype(jnp.int32) for c in PHASES)
    base = looked_up(cuts[:-1], phase)
    slots = (shift_at - base) * per_owner + tile_slot % per_owner
    late = len(PHASES)
    key = phase + ((phase == late) & (places >= FIRST_SENT)).astype(jnp.int32)
    order, bounds = grouped(key, late + 2)
    partial = None
    for p in range(late):
        (partial,) = sums(
            [arrived[s] for s in near[cuts[p] : cuts[p + 1]]],
            tiles, bounds[p], order, slots, places, owners, 0, partial, False, jnp.float32,
        )
    last = [arrived[s] for s in near[cuts[late] :]]
    ready = {}
    for g, (low, high) in enumerate([(0, FIRST_SENT), (FIRST_SENT, owners)]):
        part = sums(
            last, tiles, bounds[late + g], order, slots, places - low, high - low, low, partial,
            True, jnp.bfloat16,
        )
        for shift, block in zip(far[low:high], part):
            ready[shift] = send(block, shift)

    split = owners - LAST_PLACED
    ahead, behind = [far[-1]] + far[:split], far[split:-1]
    placed = place(ahead, owners, me, [ready[s] for s in ahead], None)
    placed = place(behind, owners, me, [ready[s] for s in behind], placed)
    return (placed.reshape(-1, feats), own_cap.reshape(-1, feats).astype(jnp.bfloat16))


def solution(mesh):
    in_specs = (
        P(GRP_BAND, None),
        P("band", None, None),
        P("band"),
        P("band"),
        P("band", None),
        P("band", None),
        P("band", None, None),
        P("band"),
        P("band"),
    )
    out_specs = (P(GRP_BAND, None), P(GRP_BAND, None))
    return jax.shard_map(
        regridded, mesh=mesh, in_specs=in_specs, out_specs=out_specs, check_vma=False
    )
```

time: 1110 us -> 842 us (0.76)
  starting transfers between devices: 24 us -> 280 us
  other arithmetic: 232 us -> 9.09 us
  waiting for transfers between devices: 627 us -> 410 us
  local copies, waits for them, and re-layouts: 124 us -> 4.17 us
  Pallas kernels: 0 us -> 115 us
  matrix products: 77.6 us -> 0 us
    all_to_all x2 -> x0, waiting for transfers between devices: 627 us -> none  [the longest x1 400 us: on_device(): lax.all_to_all(outgoing.reshape(owners, per_owner, width, feats), BAND, s...]
    ppermute x0 -> x62, waiting for transfers between devices: none -> 410 us  [send(): lax.ppermute(array, 'band', pairs(owners, shift))]
    ppermute x0 -> x62, starting transfers between devices: none -> 280 us  [send(): lax.ppermute(array, 'band', pairs(owners, shift))]
    scatter-add x9 -> x0, other arithmetic: 214 us -> none  [the longest x8 172 us: accumulate(): return (total.at[places].add(products), None)]
    pallas_call x0 -> x9, Pallas kernels: none -> 115 us  [the longest x4 78.2 us: sums(): pl.pallas_call(functools.partial(sums_kernel, len(inputs), None if before...]
    gather x10 -> x0, local copies, waits for them, and re-layouts: 81.7 us -> none  [the longest x8 60.3 us: accumulate(): inputs = arrived[slots]]
    dot_general x9 -> x0, matrix products: 77.6 us -> none  [the longest x8 66.5 us: accumulate(): jnp.einsum('tps,tsf->tpf', weights, inputs, preferred_element_type=jnp.fl...]
    all_to_all x2 -> x0, starting transfers between devices: 23.7 us -> none  [the longest x1 18.7 us: on_device(): lax.all_to_all(outgoing.reshape(owners, per_owner, width, feats), BAND, s...]
  transfers between devices with their start and end apart: 3 -> 63, of which waited for: 2 -> 28; matrix products, arithmetic and copies ran while one was open for 37% -> 1% of each run, Pallas kernels for 0% -> 11%
where the time goes in v1:
time: 842 us; the launch traced here: 833 us
  waiting for transfers between devices  410 us (49%)
  starting transfers between devices  280 us (33%)
  Pallas kernels  115 us (14%)
  between operations  14.6 us (2%)
  other arithmetic  9.09 us (1%)
    ppermute x62, waiting for transfers between devices, send(): lax.ppermute(array, 'band', pairs(owners, shift))  410 us
    ppermute x62, starting transfers between devices, send(): lax.ppermute(array, 'band', pairs(owners, shift))  280 us
    pallas_call x4, Pallas kernels, sums(): pl.pallas_call(functools.partial(sums_kernel, len(inputs), None if before...  78.2 us
    pallas_call x1, Pallas kernels, polar_sums(): pl.pallas_call(polar_kernel, out_shape=jax.ShapeDtypeStruct((blocks, widt...  21.8 us
  transfers between devices with their start and end apart: 63, of which 28 were waited for; matrix products, arithmetic and copies ran while one was open for 1% of the time, Pallas kernels for 11%

profile of v1, /device:TPU:69, one launch (start us, length us, event | category | flops | bytes accessed | tf_op | source)
XLA Modules:
  0.0 832.6 jit_solution(7630037358425574244)
XLA Ops:
  7.2 21.8 %polar.1 = f32[32,128,640]{2,1,0:T(8,128)} custom-call(s32[64]{0:T(128)} %slot_ref.1, s32[64]{0:T(128)} %place_ref.1, bf16[64,128,128]{2,1,0:T(8,128)(2,1)} %tiles_ref.9, bf16[64,128,640]{2,1,0:T(8,128)(2,1)} %bitcast.11), custom_call_target="tpu_custom_call" | custom-call | flops 1342177280 | bytes 20971520 | tf_op jit(solution)/shard_map/polar/pallas_call | solution.py:275
  32.6 10.0 %collective-permute-start.12 = (bf16[2,128,640]{2,1,0:T(8,128)(2,1)}, bf16[2,128,640]{2,1,0:T(8,128)(2,1)S(1)}, u32[]{:S(2)}, u32[]{:S(2)}) collective-permute-start(bf16[2,128,640]{2,1,0:T(8,128)(2,1)} %get-tuple-element.79), channel_id=1, source_target_pairs={{0,1},{1,0},{2,3},{3,2},{4,5},{5,4},{6,7},{7,6},{8,9},{9,8},{10,11... | collective-permute-start | bytes 983048 | tf_op jit(solution)/shard_map/ppermute | solution.py:298
  49.3 8.3 pack.2
  88.4 39.9 %collective-permute-done.2.refs_0_ = bf16[2,128,640]{2,1,0:T(8,128)(2,1)S(1)} collective-permute-done((bf16[2,128,640]{2,1,0:T(8,128)(2,1)}, bf16[2,128,640]{2,1,0:T(8,128)(2,1)S(1)}, u32[]{:S(2)}, u32[]{:S(2)}) %collective-permute-start.2) | collective-permute-done | bytes 327712 | tf_op jit(solution)/shard_map/ppermute | solution.py:298
  129.0 36.6 %collective-permute-done.4.refs_2_ = bf16[2,128,640]{2,1,0:T(8,128)(2,1)S(1)} collective-permute-done((bf16[2,128,640]{2,1,0:T(8,128)(2,1)}, bf16[2,128,640]{2,1,0:T(8,128)(2,1)S(1)}, u32[]{:S(2)}, u32[]{:S(2)}) %collective-permute-start.4) | collective-permute-done | bytes 327712 | tf_op jit(solution)/shard_map/ppermute | solution.py:298
  165.6 10.7 %collective-permute-start.19 = (bf16[2,128,640]{2,1,0:T(8,128)(2,1)}, bf16[2,128,640]{2,1,0:T(8,128)(2,1)S(1)}, u32[]{:S(2)}, u32[]{:S(2)}) collective-permute-start(bf16[2,128,640]{2,1,0:T(8,128)(2,1)} %get-tuple-element.86), channel_id=1, source_target_pairs={{0,5},{1,4},{2,7},{3,6},{4,9},{5,8},{6,11},{7,10},{8,13},{9,12},{1... | collective-permute-start | bytes 983048 | tf_op jit(solution)/shard_map/ppermute | solution.py:298
  176.3 46.6 %collective-permute-done.6.refs_4_ = bf16[2,128,640]{2,1,0:T(8,128)(2,1)S(1)} collective-permute-done((bf16[2,128,640]{2,1,0:T(8,128)(2,1)}, bf16[2,128,640]{2,1,0:T(8,128)(2,1)S(1)}, u32[]{:S(2)}, u32[]{:S(2)}) %collective-permute-start.6) | collective-permute-done | bytes 327712 | tf_op jit(solution)/shard_map/ppermute | solution.py:298
  224.8 30.4 %collective-permute-done.8.refs_6_ = bf16[2,128,640]{2,1,0:T(8,128)(2,1)S(1)} collective-permute-done((bf16[2,128,640]{2,1,0:T(8,128)(2,1)}, bf16[2,128,640]{2,1,0:T(8,128)(2,1)S(1)}, u32[]{:S(2)}, u32[]{:S(2)}) %collective-permute-start.8) | collective-permute-done | bytes 327712 | tf_op jit(solution)/shard_map/ppermute | solution.py:298
  255.1 12.0 %collective-permute-start.22 = (bf16[2,128,640]{2,1,0:T(8,128)(2,1)}, bf16[2,128,640]{2,1,0:T(8,128)(2,1)S(1)}, u32[]{:S(2)}, u32[]{:S(2)}) collective-permute-start(bf16[2,128,640]{2,1,0:T(8,128)(2,1)} %get-tuple-element.89), channel_id=1, source_target_pairs={{0,26},{1,27},{2,28},{3,29},{4,30},{5,31},{6,0},{7,1},{8,2},{9,3},... | collective-permute-start | bytes 983048 | tf_op jit(solution)/shard_map/ppermute | solution.py:298
  273.6 11.1 %collective-permute-done.19.refs_8_ = bf16[2,128,640]{2,1,0:T(8,128)(2,1)S(1)} collective-permute-done((bf16[2,128,640]{2,1,0:T(8,128)(2,1)}, bf16[2,128,640]{2,1,0:T(8,128)(2,1)S(1)}, u32[]{:S(2)}, u32[]{:S(2)}) %collective-permute-start.19) | collective-permute-done | bytes 327712 | tf_op jit(solution)/shard_map/ppermute | solution.py:298
  287.5 21.3 %collective-permute-done.21.refs_10_ = bf16[2,128,640]{2,1,0:T(8,128)(2,1)S(1)} collective-permute-done((bf16[2,128,640]{2,1,0:T(8,128)(2,1)}, bf16[2,128,640]{2,1,0:T(8,128)(2,1)S(1)}, u32[]{:S(2)}, u32[]{:S(2)}) %collective-permute-start.21) | collective-permute-done | bytes 327712 | tf_op jit(solution)/shard_map/ppermute | solution.py:298
  309.4 9.5 %collective-permute-start.27 = (bf16[2,128,640]{2,1,0:T(8,128)(2,1)}, bf16[2,128,640]{2,1,0:T(8,128)(2,1)S(1)}, u32[]{:S(2)}, u32[]{:S(2)}) collective-permute-start(bf16[2,128,640]{2,1,0:T(8,128)(2,1)} %get-tuple-element.94), channel_id=1, source_target_pairs={{0,9},{1,8},{2,11},{3,10},{4,13},{5,12},{6,15},{7,14},{8,17},{9,16... | collective-permute-start | bytes 983048 | tf_op jit(solution)/shard_map/ppermute | solution.py:298
  318.9 17.0 %collective-permute-done.23.refs_12_ = bf16[2,128,640]{2,1,0:T(8,128)(2,1)S(1)} collective-permute-done((bf16[2,128,640]{2,1,0:T(8,128)(2,1)}, bf16[2,128,640]{2,1,0:T(8,128)(2,1)S(1)}, u32[]{:S(2)}, u32[]{:S(2)}) %collective-permute-start.23) | collective-permute-done | bytes 327712 | tf_op jit(solution)/shard_map/ppermute | solution.py:298
  343.0 19.7 %collective-permute-done.25.refs_14_ = bf16[2,128,640]{2,1,0:T(8,128)(2,1)S(1)} collective-permute-done((bf16[2,128,640]{2,1,0:T(8,128)(2,1)}, bf16[2,128,640]{2,1,0:T(8,128)(2,1)S(1)}, u32[]{:S(2)}, u32[]{:S(2)}) %collective-permute-start.25) | collective-permute-done | bytes 327712 | tf_op jit(solution)/shard_map/ppermute | solution.py:298
  362.7 8.5 %collective-permute-start.30 = (bf16[2,128,640]{2,1,0:T(8,128)(2,1)}, bf16[2,128,640]{2,1,0:T(8,128)(2,1)S(1)}, u32[]{:S(2)}, u32[]{:S(2)}) collective-permute-start(bf16[2,128,640]{2,1,0:T(8,128)(2,1)} %get-tuple-element.97), channel_id=1, source_target_pairs={{0,22},{1,23},{2,24},{3,25},{4,26},{5,27},{6,28},{7,29},{8,30},{9,... | collective-permute-start | bytes 983048 | tf_op jit(solution)/shard_map/ppermute | solution.py:298
  373.4 26.7 %collective-permute-done.27.refs_16_ = bf16[2,128,640]{2,1,0:T(8,128)(2,1)S(1)} collective-permute-done((bf16[2,128,640]{2,1,0:T(8,128)(2,1)}, bf16[2,128,640]{2,1,0:T(8,128)(2,1)S(1)}, u32[]{:S(2)}, u32[]{:S(2)}) %collective-permute-start.27) | collective-permute-done | bytes 327712 | tf_op jit(solution)/shard_map/ppermute | solution.py:298
  400.2 9.5 %collective-permute-start.11 = (bf16[2,128,640]{2,1,0:T(8,128)(2,1)}, bf16[2,128,640]{2,1,0:T(8,128)(2,1)S(1)}, u32[]{:S(2)}, u32[]{:S(2)}) collective-permute-start(bf16[2,128,640]{2,1,0:T(8,128)(2,1)} %get-tuple-element.77), channel_id=1, source_target_pairs={{0,19},{1,18},{2,21},{3,20},{4,23},{5,22},{6,25},{7,24},{8,27},{9,... | collective-permute-start | bytes 983048 | tf_op jit(solution)/shard_map/ppermute | solution.py:298
  411.0 21.9 %collective-permute-done.29.refs_18_ = bf16[2,128,640]{2,1,0:T(8,128)(2,1)S(1)} collective-permute-done((bf16[2,128,640]{2,1,0:T(8,128)(2,1)}, bf16[2,128,640]{2,1,0:T(8,128)(2,1)S(1)}, u32[]{:S(2)}, u32[]{:S(2)}) %collective-permute-start.29) | collective-permute-done | bytes 327712 | tf_op jit(solution)/shard_map/ppermute | solution.py:298
  432.9 11.6 %collective-permute-start = (bf16[2,128,640]{2,1,0:T(8,128)(2,1)}, bf16[2,128,640]{2,1,0:T(8,128)(2,1)S(1)}, u32[]{:S(2)}, u32[]{:S(2)}) collective-permute-start(bf16[2,128,640]{2,1,0:T(8,128)(2,1)} %get-tuple-element.66), channel_id=1, source_target_pairs={{0,16},{1,17},{2,18},{3,19},{4,20},{5,21},{6,22},{7,23},{8,24},{9,... | collective-permute-start | bytes 983048 | tf_op jit(solution)/shard_map/ppermute | solution.py:298
  444.5 21.9 %collective-permute-start.1 = (bf16[2,128,640]{2,1,0:T(8,128)(2,1)}, bf16[2,128,640]{2,1,0:T(8,128)(2,1)S(1)}, u32[]{:S(2)}, u32[]{:S(2)}) collective-permute-start(bf16[2,128,640]{2,1,0:T(8,128)(2,1)} %get-tuple-element.67), channel_id=1, source_target_pairs={{0,17},{1,16},{2,19},{3,18},{4,21},{5,20},{6,23},{7,22},{8,25},{9,... | collective-permute-start | bytes 983048 | tf_op jit(solution)/shard_map/ppermute | solution.py:298
  466.5 37.0 %shard_map.131.refs_10_ = f32[32,128,640]{2,1,0:T(8,128)} custom-call(s32[2]{0:T(128)} %pad_add_fusion.2.bounds_ref, s32[256]{0:T(256)} %select_reduce_fusion.order_ref, s32[256]{0:T(256)} %get-tuple-element.136.slot_ref, s32[256]{0:T(256)} %copy-done.3, bf16[256,128,128]{2,1,0:T(8,128)(2,1)} %tiles_ref.8, bf16[2,128,640]{2,1,0:T(8,128)(2,1)} %get-tuple-element.78.refs_0_, ...), custom_call_target="tpu_custom_call" | custom-call | flops 3355443200 | bytes 15728640 | tf_op jit(solution)/shard_map/pallas_call | solution.py:183
  503.6 51.3 %collective-permute-done.11.refs_9_ = bf16[2,128,640]{2,1,0:T(8,128)(2,1)S(1)} collective-permute-done((bf16[2,128,640]{2,1,0:T(8,128)(2,1)}, bf16[2,128,640]{2,1,0:T(8,128)(2,1)S(1)}, u32[]{:S(2)}, u32[]{:S(2)}) %collective-permute-start.11) | collective-permute-done | bytes 327712 | tf_op jit(solution)/shard_map/ppermute | solution.py:298
  559.0 30.7 %shard_map.132.refs_2_ = f32[32,128,640]{2,1,0:T(8,128)} custom-call(s32[2]{0:T(128)S(1)} %pad_add_fusion.1.bounds_ref, s32[256]{0:T(256)S(1)} %copy-done.2, s32[256]{0:T(256)S(1)} %copy-done.1, s32[256]{0:T(256)S(1)} %copy-done.4, bf16[256,128,128]{2,1,0:T(8,128)(2,1)S(1)} %copy-done, bf16[2,128,640]{2,1,0:T(8,128)(2,1)S(1)} %collective-permute-done.2.refs_0_, ...), custom_call_target="tpu_custom_call" | custom-call | flops 1677721600 | bytes 15728640 | tf_op jit(solution)/shard_map/pallas_call | solution.py:183
  599.8 14.2 %collective-permute-start.33 = (bf16[128,640]{1,0:T(8,128)(2,1)S(1)}, bf16[128,640]{1,0:T(8,128)(2,1)S(1)}, u32[]{:S(2)}, u32[]{:S(2)}) collective-permute-start(bf16[128,640]{1,0:T(8,128)(2,1)S(1)} %get-tuple-element.101), channel_id=1, source_target_pairs={{0,19},{1,18},{2,21},{3,20},{4,23},{5,22},{6,25},{7,24},{8,27},{9,... | collective-permute-start | bytes 491528 | tf_op jit(solution)/shard_map/ppermute | solution.py:298
  614.0 9.4 %collective-permute-start.35 = (bf16[128,640]{1,0:T(8,128)(2,1)S(1)}, bf16[128,640]{1,0:T(8,128)(2,1)S(1)}, u32[]{:S(2)}, u32[]{:S(2)}) collective-permute-start(bf16[128,640]{1,0:T(8,128)(2,1)S(1)} %get-tuple-element.103), channel_id=1, source_target_pairs={{0,18},{1,19},{2,20},{3,21},{4,22},{5,23},{6,24},{7,25},{8,26},{9,... | collective-permute-start | bytes 491528 | tf_op jit(solution)/shard_map/ppermute | solution.py:298
  630.3 9.2 %collective-permute-start.37 = (bf16[128,640]{1,0:T(8,128)(2,1)S(1)}, bf16[128,640]{1,0:T(8,128)(2,1)S(1)}, u32[]{:S(2)}, u32[]{:S(2)}) collective-permute-start(bf16[128,640]{1,0:T(8,128)(2,1)S(1)} %get-tuple-element.105), channel_id=1, source_target_pairs={{0,21},{1,20},{2,23},{3,22},{4,25},{5,24},{6,27},{7,26},{8,29},{9,... | collective-permute-start | bytes 491528 | tf_op jit(solution)/shard_map/ppermute | solution.py:298
  639.5 18.4 %collective-permute-done.33.refs_3_ = bf16[128,640]{1,0:T(8,128)(2,1)S(1)} collective-permute-done((bf16[128,640]{1,0:T(8,128)(2,1)S(1)}, bf16[128,640]{1,0:T(8,128)(2,1)S(1)}, u32[]{:S(2)}, u32[]{:S(2)}) %collective-permute-start.33) | collective-permute-done | bytes 163872 | tf_op jit(solution)/shard_map/ppermute | solution.py:298
  670.5 10.7 %collective-permute-start.40 = (bf16[128,640]{1,0:T(8,128)(2,1)S(1)}, bf16[128,640]{1,0:T(8,128)(2,1)S(1)}, u32[]{:S(2)}, u32[]{:S(2)}) collective-permute-start(bf16[128,640]{1,0:T(8,128)(2,1)S(1)} %get-tuple-element.108), channel_id=1, source_target_pairs={{0,12},{1,13},{2,14},{3,15},{4,16},{5,17},{6,18},{7,19},{8,20},{9,... | collective-permute-start | bytes 491528 | tf_op jit(solution)/shard_map/ppermute | solution.py:298
  681.2 15.2 %collective-permute-start.41 = (bf16[128,640]{1,0:T(8,128)(2,1)S(1)}, bf16[128,640]{1,0:T(8,128)(2,1)S(1)}, u32[]{:S(2)}, u32[]{:S(2)}) collective-permute-start(bf16[128,640]{1,0:T(8,128)(2,1)S(1)} %get-tuple-element.109), channel_id=1, source_target_pairs={{0,23},{1,22},{2,25},{3,24},{4,27},{5,26},{6,29},{7,28},{8,31},{9,... | collective-permute-start | bytes 491528 | tf_op jit(solution)/shard_map/ppermute | solution.py:298
  696.3 14.9 %collective-permute-done.37.refs_7_ = bf16[128,640]{1,0:T(8,128)(2,1)S(1)} collective-permute-done((bf16[128,640]{1,0:T(8,128)(2,1)S(1)}, bf16[128,640]{1,0:T(8,128)(2,1)S(1)}, u32[]{:S(2)}, u32[]{:S(2)}) %collective-permute-start.37) | collective-permute-done | bytes 163872 | tf_op jit(solution)/shard_map/ppermute | solution.py:298
  724.9 10.1 %collective-permute-start.45 = (bf16[128,640]{1,0:T(8,128)(2,1)S(1)}, bf16[128,640]{1,0:T(8,128)(2,1)S(1)}, u32[]{:S(2)}, u32[]{:S(2)}) collective-permute-start(bf16[128,640]{1,0:T(8,128)(2,1)S(1)} %get-tuple-element.113), channel_id=1, source_target_pairs={{0,25},{1,24},{2,27},{3,26},{4,29},{5,28},{6,31},{7,30},{8,1},{9,0... | collective-permute-start | bytes 491528 | tf_op jit(solution)/shard_map/ppermute | solution.py:298
  746.9 21.5 %collective-permute-start.48 = (bf16[128,640]{1,0:T(8,128)(2,1)S(1)}, bf16[128,640]{1,0:T(8,128)(2,1)S(1)}, u32[]{:S(2)}, u32[]{:S(2)}) collective-permute-start(bf16[128,640]{1,0:T(8,128)(2,1)S(1)} %get-tuple-element.116), channel_id=1, source_target_pairs={{0,8},{1,9},{2,10},{3,11},{4,12},{5,13},{6,14},{7,15},{8,16},{9,17... | collective-permute-start | bytes 491528 | tf_op jit(solution)/shard_map/ppermute | solution.py:298
  (182 shorter events, 180.4 us)
Async XLA Ops:
  7.2 816.9 %reduce-scatter.2.cloned.1.call-start = ((), (), s32[]{:S(2)}) async-start(), calls=%async_computation.1 | async-start | bytes 10813440 | tf_op jit(solution)/shard_map/reduce_scatter | solution.py:309
  58.0 70.3 %collective-permute-start.2 = (bf16[2,128,640]{2,1,0:T(8,128)(2,1)}, bf16[2,128,640]{2,1,0:T(8,128)(2,1)S(1)}, u32[]{:S(2)}, u32[]{:S(2)}) collective-permute-start(bf16[2,128,640]{2,1,0:T(8,128)(2,1)} %get-tuple-element.68), channel_id=1, source_target_pairs={{0,11},{1,10},{2,13},{3,12},{4,15},{5,14},{6,17},{7,16},{8,19},{9,... | collective-permute-start | bytes 983048 | tf_op jit(solution)/shard_map/ppermute | solution.py:298
  61.5 66.8 %collective-permute-start.3 = (bf16[2,128,640]{2,1,0:T(8,128)(2,1)}, bf16[2,128,640]{2,1,0:T(8,128)(2,1)S(1)}, u32[]{:S(2)}, u32[]{:S(2)}) collective-permute-start(bf16[2,128,640]{2,1,0:T(8,128)(2,1)} %get-tuple-element.69), channel_id=1, source_target_pairs={{0,23},{1,22},{2,25},{3,24},{4,27},{5,26},{6,29},{7,28},{8,31},{9,... | collective-permute-start | bytes 983048 | tf_op jit(solution)/shard_map/ppermute | solution.py:298
  66.7 99.0 %collective-permute-start.4 = (bf16[2,128,640]{2,1,0:T(8,128)(2,1)}, bf16[2,128,640]{2,1,0:T(8,128)(2,1)S(1)}, u32[]{:S(2)}, u32[]{:S(2)}) collective-permute-start(bf16[2,128,640]{2,1,0:T(8,128)(2,1)} %get-tuple-element.70), channel_id=1, source_target_pairs={{0,12},{1,13},{2,14},{3,15},{4,16},{5,17},{6,18},{7,19},{8,20},{9,... | collective-permute-start | bytes 983048 | tf_op jit(solution)/shard_map/ppermute | solution.py:298
  70.3 95.3 %collective-permute-start.5 = (bf16[2,128,640]{2,1,0:T(8,128)(2,1)}, bf16[2,128,640]{2,1,0:T(8,128)(2,1)S(1)}, u32[]{:S(2)}, u32[]{:S(2)}) collective-permute-start(bf16[2,128,640]{2,1,0:T(8,128)(2,1)} %get-tuple-element.71), channel_id=1, source_target_pairs={{0,20},{1,21},{2,22},{3,23},{4,24},{5,25},{6,26},{7,27},{8,28},{9,... | collective-permute-start | bytes 983048 | tf_op jit(solution)/shard_map/ppermute | solution.py:298
  83.2 139.8 %collective-permute-start.6 = (bf16[2,128,640]{2,1,0:T(8,128)(2,1)}, bf16[2,128,640]{2,1,0:T(8,128)(2,1)S(1)}, u32[]{:S(2)}, u32[]{:S(2)}) collective-permute-start(bf16[2,128,640]{2,1,0:T(8,128)(2,1)} %get-tuple-element.72), channel_id=1, source_target_pairs={{0,13},{1,12},{2,15},{3,14},{4,17},{5,16},{6,19},{7,18},{8,21},{9,... | collective-permute-start | bytes 983048 | tf_op jit(solution)/shard_map/ppermute | solution.py:298
  128.3 94.7 %collective-permute-start.7 = (bf16[2,128,640]{2,1,0:T(8,128)(2,1)}, bf16[2,128,640]{2,1,0:T(8,128)(2,1)S(1)}, u32[]{:S(2)}, u32[]{:S(2)}) collective-permute-start(bf16[2,128,640]{2,1,0:T(8,128)(2,1)} %get-tuple-element.73), channel_id=1, source_target_pairs={{0,21},{1,20},{2,23},{3,22},{4,25},{5,24},{6,27},{7,26},{8,29},{9,... | collective-permute-start | bytes 983048 | tf_op jit(solution)/shard_map/ppermute | solution.py:298
  128.3 126.8 %collective-permute-start.8 = (bf16[2,128,640]{2,1,0:T(8,128)(2,1)}, bf16[2,128,640]{2,1,0:T(8,128)(2,1)S(1)}, u32[]{:S(2)}, u32[]{:S(2)}) collective-permute-start(bf16[2,128,640]{2,1,0:T(8,128)(2,1)} %get-tuple-element.74), channel_id=1, source_target_pairs={{0,14},{1,15},{2,16},{3,17},{4,18},{5,19},{6,20},{7,21},{8,22},{9,... | collective-permute-start | bytes 983048 | tf_op jit(solution)/shard_map/ppermute | solution.py:298
  165.6 101.5 %collective-permute-start.18 = (bf16[2,128,640]{2,1,0:T(8,128)(2,1)}, bf16[2,128,640]{2,1,0:T(8,128)(2,1)S(1)}, u32[]{:S(2)}, u32[]{:S(2)}) collective-permute-start(bf16[2,128,640]{2,1,0:T(8,128)(2,1)} %get-tuple-element.85), channel_id=1, source_target_pairs={{0,28},{1,29},{2,30},{3,31},{4,0},{5,1},{6,2},{7,3},{8,4},{9,5},{1... | collective-permute-start | bytes 983048 | tf_op jit(solution)/shard_map/ppermute | solution.py:298
  165.6 119.0 %collective-permute-start.19 = (bf16[2,128,640]{2,1,0:T(8,128)(2,1)}, bf16[2,128,640]{2,1,0:T(8,128)(2,1)S(1)}, u32[]{:S(2)}, u32[]{:S(2)}) collective-permute-start(bf16[2,128,640]{2,1,0:T(8,128)(2,1)} %get-tuple-element.86), channel_id=1, source_target_pairs={{0,5},{1,4},{2,7},{3,6},{4,9},{5,8},{6,11},{7,10},{8,13},{9,12},{1... | collective-permute-start | bytes 983048 | tf_op jit(solution)/shard_map/ppermute | solution.py:298
  222.9 63.0 %collective-permute-start.20 = (bf16[2,128,640]{2,1,0:T(8,128)(2,1)}, bf16[2,128,640]{2,1,0:T(8,128)(2,1)S(1)}, u32[]{:S(2)}, u32[]{:S(2)}) collective-permute-start(bf16[2,128,640]{2,1,0:T(8,128)(2,1)} %get-tuple-element.87), channel_id=1, source_target_pairs={{0,29},{1,28},{2,31},{3,30},{4,1},{5,0},{6,3},{7,2},{8,5},{9,4},{1... | collective-permute-start | bytes 983048 | tf_op jit(solution)/shard_map/ppermute | solution.py:298
  223.0 85.8 %collective-permute-start.21 = (bf16[2,128,640]{2,1,0:T(8,128)(2,1)}, bf16[2,128,640]{2,1,0:T(8,128)(2,1)S(1)}, u32[]{:S(2)}, u32[]{:S(2)}) collective-permute-start(bf16[2,128,640]{2,1,0:T(8,128)(2,1)} %get-tuple-element.88), channel_id=1, source_target_pairs={{0,6},{1,7},{2,8},{3,9},{4,10},{5,11},{6,12},{7,13},{8,14},{9,15},... | collective-permute-start | bytes 983048 | tf_op jit(solution)/shard_map/ppermute | solution.py:298
  255.1 54.3 %collective-permute-start.22 = (bf16[2,128,640]{2,1,0:T(8,128)(2,1)}, bf16[2,128,640]{2,1,0:T(8,128)(2,1)S(1)}, u32[]{:S(2)}, u32[]{:S(2)}) collective-permute-start(bf16[2,128,640]{2,1,0:T(8,128)(2,1)} %get-tuple-element.89), channel_id=1, source_target_pairs={{0,26},{1,27},{2,28},{3,29},{4,30},{5,31},{6,0},{7,1},{8,2},{9,3},... | collective-permute-start | bytes 983048 | tf_op jit(solution)/shard_map/ppermute | solution.py:298
  267.1 68.8 %collective-permute-start.23 = (bf16[2,128,640]{2,1,0:T(8,128)(2,1)}, bf16[2,128,640]{2,1,0:T(8,128)(2,1)S(1)}, u32[]{:S(2)}, u32[]{:S(2)}) collective-permute-start(bf16[2,128,640]{2,1,0:T(8,128)(2,1)} %get-tuple-element.90), channel_id=1, source_target_pairs={{0,7},{1,6},{2,9},{3,8},{4,11},{5,10},{6,13},{7,12},{8,15},{9,14},... | collective-permute-start | bytes 983048 | tf_op jit(solution)/shard_map/ppermute | solution.py:298
  285.9 76.7 %collective-permute-start.25 = (bf16[2,128,640]{2,1,0:T(8,128)(2,1)}, bf16[2,128,640]{2,1,0:T(8,128)(2,1)S(1)}, u32[]{:S(2)}, u32[]{:S(2)}) collective-permute-start(bf16[2,128,640]{2,1,0:T(8,128)(2,1)} %get-tuple-element.92), channel_id=1, source_target_pairs={{0,8},{1,9},{2,10},{3,11},{4,12},{5,13},{6,14},{7,15},{8,16},{9,17... | collective-permute-start | bytes 983048 | tf_op jit(solution)/shard_map/ppermute | solution.py:298
  308.8 64.4 %collective-permute-start.26 = (bf16[2,128,640]{2,1,0:T(8,128)(2,1)}, bf16[2,128,640]{2,1,0:T(8,128)(2,1)S(1)}, u32[]{:S(2)}, u32[]{:S(2)}) collective-permute-start(bf16[2,128,640]{2,1,0:T(8,128)(2,1)} %get-tuple-element.93), channel_id=1, source_target_pairs={{0,24},{1,25},{2,26},{3,27},{4,28},{5,29},{6,30},{7,31},{8,0},{9,1... | collective-permute-start | bytes 983048 | tf_op jit(solution)/shard_map/ppermute | solution.py:298
  309.4 90.7 %collective-permute-start.27 = (bf16[2,128,640]{2,1,0:T(8,128)(2,1)}, bf16[2,128,640]{2,1,0:T(8,128)(2,1)S(1)}, u32[]{:S(2)}, u32[]{:S(2)}) collective-permute-start(bf16[2,128,640]{2,1,0:T(8,128)(2,1)} %get-tuple-element.94), channel_id=1, source_target_pairs={{0,9},{1,8},{2,11},{3,10},{4,13},{5,12},{6,15},{7,14},{8,17},{9,16... | collective-permute-start | bytes 983048 | tf_op jit(solution)/shard_map/ppermute | solution.py:298
  335.9 64.2 %collective-permute-start.28 = (bf16[2,128,640]{2,1,0:T(8,128)(2,1)}, bf16[2,128,640]{2,1,0:T(8,128)(2,1)S(1)}, u32[]{:S(2)}, u32[]{:S(2)}) collective-permute-start(bf16[2,128,640]{2,1,0:T(8,128)(2,1)} %get-tuple-element.95), channel_id=1, source_target_pairs={{0,25},{1,24},{2,27},{3,26},{4,29},{5,28},{6,31},{7,30},{8,1},{9,0... | collective-permute-start | bytes 983048 | tf_op jit(solution)/shard_map/ppermute | solution.py:298
  338.1 94.9 %collective-permute-start.29 = (bf16[2,128,640]{2,1,0:T(8,128)(2,1)}, bf16[2,128,640]{2,1,0:T(8,128)(2,1)S(1)}, u32[]{:S(2)}, u32[]{:S(2)}) collective-permute-start(bf16[2,128,640]{2,1,0:T(8,128)(2,1)} %get-tuple-element.96), channel_id=1, source_target_pairs={{0,10},{1,11},{2,12},{3,13},{4,14},{5,15},{6,16},{7,17},{8,18},{9,... | collective-permute-start | bytes 983048 | tf_op jit(solution)/shard_map/ppermute | solution.py:298
  362.7 81.9 %collective-permute-start.30 = (bf16[2,128,640]{2,1,0:T(8,128)(2,1)}, bf16[2,128,640]{2,1,0:T(8,128)(2,1)S(1)}, u32[]{:S(2)}, u32[]{:S(2)}) collective-permute-start(bf16[2,128,640]{2,1,0:T(8,128)(2,1)} %get-tuple-element.97), channel_id=1, source_target_pairs={{0,22},{1,23},{2,24},{3,25},{4,26},{5,27},{6,28},{7,29},{8,30},{9,... | collective-permute-start | bytes 983048 | tf_op jit(solution)/shard_map/ppermute | solution.py:298
  373.3 130.3 %collective-permute-start.9 = (bf16[2,128,640]{2,1,0:T(8,128)(2,1)}, bf16[2,128,640]{2,1,0:T(8,128)(2,1)S(1)}, u32[]{:S(2)}, u32[]{:S(2)}) collective-permute-start(bf16[2,128,640]{2,1,0:T(8,128)(2,1)} %get-tuple-element.75), channel_id=1, source_target_pairs={{0,18},{1,19},{2,20},{3,21},{4,22},{5,23},{6,24},{7,25},{8,26},{9,... | collective-permute-start | bytes 983048 | tf_op jit(solution)/shard_map/ppermute | solution.py:298
  400.1 103.5 %collective-permute-start.10 = (bf16[2,128,640]{2,1,0:T(8,128)(2,1)}, bf16[2,128,640]{2,1,0:T(8,128)(2,1)S(1)}, u32[]{:S(2)}, u32[]{:S(2)}) collective-permute-start(bf16[2,128,640]{2,1,0:T(8,128)(2,1)} %get-tuple-element.76), channel_id=1, source_target_pairs={{0,15},{1,14},{2,17},{3,16},{4,19},{5,18},{6,21},{7,20},{8,23},{9,... | collective-permute-start | bytes 983048 | tf_op jit(solution)/shard_map/ppermute | solution.py:298
  400.2 154.8 %collective-permute-start.11 = (bf16[2,128,640]{2,1,0:T(8,128)(2,1)}, bf16[2,128,640]{2,1,0:T(8,128)(2,1)S(1)}, u32[]{:S(2)}, u32[]{:S(2)}) collective-permute-start(bf16[2,128,640]{2,1,0:T(8,128)(2,1)} %get-tuple-element.77), channel_id=1, source_target_pairs={{0,19},{1,18},{2,21},{3,20},{4,23},{5,22},{6,25},{7,24},{8,27},{9,... | collective-permute-start | bytes 983048 | tf_op jit(solution)/shard_map/ppermute | solution.py:298
  432.9 156.8 %collective-permute-start = (bf16[2,128,640]{2,1,0:T(8,128)(2,1)}, bf16[2,128,640]{2,1,0:T(8,128)(2,1)S(1)}, u32[]{:S(2)}, u32[]{:S(2)}) collective-permute-start(bf16[2,128,640]{2,1,0:T(8,128)(2,1)} %get-tuple-element.66), channel_id=1, source_target_pairs={{0,16},{1,17},{2,18},{3,19},{4,20},{5,21},{6,22},{7,23},{8,24},{9,... | collective-permute-start | bytes 983048 | tf_op jit(solution)/shard_map/ppermute | solution.py:298
  444.5 145.2 %collective-permute-start.1 = (bf16[2,128,640]{2,1,0:T(8,128)(2,1)}, bf16[2,128,640]{2,1,0:T(8,128)(2,1)S(1)}, u32[]{:S(2)}, u32[]{:S(2)}) collective-permute-start(bf16[2,128,640]{2,1,0:T(8,128)(2,1)} %get-tuple-element.67), channel_id=1, source_target_pairs={{0,17},{1,16},{2,19},{3,18},{4,21},{5,20},{6,23},{7,22},{8,25},{9,... | collective-permute-start | bytes 983048 | tf_op jit(solution)/shard_map/ppermute | solution.py:298
  599.8 58.1 %collective-permute-start.33 = (bf16[128,640]{1,0:T(8,128)(2,1)S(1)}, bf16[128,640]{1,0:T(8,128)(2,1)S(1)}, u32[]{:S(2)}, u32[]{:S(2)}) collective-permute-start(bf16[128,640]{1,0:T(8,128)(2,1)S(1)} %get-tuple-element.101), channel_id=1, source_target_pairs={{0,19},{1,18},{2,21},{3,20},{4,23},{5,22},{6,25},{7,24},{8,27},{9,... | collective-permute-start | bytes 491528 | tf_op jit(solution)/shard_map/ppermute | solution.py:298
  614.0 56.5 %collective-permute-start.35 = (bf16[128,640]{1,0:T(8,128)(2,1)S(1)}, bf16[128,640]{1,0:T(8,128)(2,1)S(1)}, u32[]{:S(2)}, u32[]{:S(2)}) collective-permute-start(bf16[128,640]{1,0:T(8,128)(2,1)S(1)} %get-tuple-element.103), channel_id=1, source_target_pairs={{0,18},{1,19},{2,20},{3,21},{4,22},{5,23},{6,24},{7,25},{8,26},{9,... | collective-permute-start | bytes 491528 | tf_op jit(solution)/shard_map/ppermute | solution.py:298
  623.4 57.7 %collective-permute-start.36 = (bf16[128,640]{1,0:T(8,128)(2,1)S(1)}, bf16[128,640]{1,0:T(8,128)(2,1)S(1)}, u32[]{:S(2)}, u32[]{:S(2)}) collective-permute-start(bf16[128,640]{1,0:T(8,128)(2,1)S(1)} %get-tuple-element.104), channel_id=1, source_target_pairs={{0,14},{1,15},{2,16},{3,17},{4,18},{5,19},{6,20},{7,21},{8,22},{9,... | collective-permute-start | bytes 491528 | tf_op jit(solution)/shard_map/ppermute | solution.py:298
  630.3 80.9 %collective-permute-start.37 = (bf16[128,640]{1,0:T(8,128)(2,1)S(1)}, bf16[128,640]{1,0:T(8,128)(2,1)S(1)}, u32[]{:S(2)}, u32[]{:S(2)}) collective-permute-start(bf16[128,640]{1,0:T(8,128)(2,1)S(1)} %get-tuple-element.105), channel_id=1, source_target_pairs={{0,21},{1,20},{2,23},{3,22},{4,25},{5,24},{6,27},{7,26},{8,29},{9,... | collective-permute-start | bytes 491528 | tf_op jit(solution)/shard_map/ppermute | solution.py:298
  662.3 62.6 %collective-permute-start.39 = (bf16[128,640]{1,0:T(8,128)(2,1)S(1)}, bf16[128,640]{1,0:T(8,128)(2,1)S(1)}, u32[]{:S(2)}, u32[]{:S(2)}) collective-permute-start(bf16[128,640]{1,0:T(8,128)(2,1)S(1)} %get-tuple-element.107), channel_id=1, source_target_pairs={{0,20},{1,21},{2,22},{3,23},{4,24},{5,25},{6,26},{7,27},{8,28},{9,... | collective-permute-start | bytes 491528 | tf_op jit(solution)/shard_map/ppermute | solution.py:298
  670.5 54.5 %collective-permute-start.40 = (bf16[128,640]{1,0:T(8,128)(2,1)S(1)}, bf16[128,640]{1,0:T(8,128)(2,1)S(1)}, u32[]{:S(2)}, u32[]{:S(2)}) collective-permute-start(bf16[128,640]{1,0:T(8,128)(2,1)S(1)} %get-tuple-element.108), channel_id=1, source_target_pairs={{0,12},{1,13},{2,14},{3,15},{4,16},{5,17},{6,18},{7,19},{8,20},{9,... | collective-permute-start | bytes 491528 | tf_op jit(solution)/shard_map/ppermute | solution.py:298
  681.2 53.9 %collective-permute-start.41 = (bf16[128,640]{1,0:T(8,128)(2,1)S(1)}, bf16[128,640]{1,0:T(8,128)(2,1)S(1)}, u32[]{:S(2)}, u32[]{:S(2)}) collective-permute-start(bf16[128,640]{1,0:T(8,128)(2,1)S(1)} %get-tuple-element.109), channel_id=1, source_target_pairs={{0,23},{1,22},{2,25},{3,24},{4,27},{5,26},{6,29},{7,28},{8,31},{9,... | collective-permute-start | bytes 491528 | tf_op jit(solution)/shard_map/ppermute | solution.py:298
  (63 other events, 5434.1 us)
Sparse Core Ops, SparseCore 0:
  29.3 539.3 reduce-scatter.1

commit v2 on v1

--- a/solution.py
+++ b/solution.py
@@ -11,8 +11,8 @@
 
 GRP_BAND = ("grp", "band")
 CORES = 2
-FIRST_PACK = 7
-PHASES = (20, 30)
+FIRST_PACK = 3
+PHASES = (18, 28)
 FIRST_SENT = 8
 LAST_PLACED = 8
 ANY = pl.BlockSpec(memory_space=pl.ANY)
@@ -32,6 +32,13 @@
     chips = owners // CORES
     shifts = [(d, c) for d in range(chips) for c in range(CORES)]
     return sorted(shifts, key=lambda s: (min(s[0], chips - s[0]), s[1], s[0]))
+
+
+def sending_order(owners):
+    near = near_to_far(owners)
+    hop = owners // CORES // 2 - 1
+    long = [s for s in near if s[0] in (hop, hop + 2) and s[1] == 0]
+    return near[:1] + long + [s for s in near[1:] if s not in long]
 
 
 def pairs(owners, shift):
@@ -297,7 +304,7 @@
     def send(array, shift):
         return array if shift == (0, 0) else lax.ppermute(array, "band", pairs(owners, shift))
 
-    near = near_to_far(owners)
+    near = sending_order(owners)
     own, first, rest = near[:1], near[1:FIRST_PACK], near[FIRST_PACK:]
     arrived = {}
     for part in (first, rest + own):
@@ -308,9 +315,8 @@
     cap_part = polar_sums(polar_tiles, polar_src, polar_dst, blocks, owners)
     own_cap = lax.psum_scatter(cap_part, "band", scatter_dimension=0, tiled=True)
 
-    far = near[::-1]
-    rows = [s[0] * CORES + s[1] for s in near]
-    near_at, far_at = np.argsort(rows), np.argsort(rows[::-1])
+    far = near_to_far(owners)[::-1]
+    near_at, far_at = (np.argsort([s[0] * CORES + s[1] for s in x]) for x in (near, far))
     cuts = (0, *PHASES, owners)
     shift_at = looked_up(near_at, apart(owners, tile_slot // per_owner, here))
     places = looked_up(far_at, apart(owners, here, tile_dst))

time: 842 us -> 858 us (1.019)
  starting transfers between devices: 280 us -> 399 us
  waiting for transfers between devices: 410 us -> 310 us
    ppermute x62, starting transfers between devices: 280 us -> 399 us  [send(): lax.ppermute(array, 'band', pairs(owners, shift))]
    ppermute x62, waiting for transfers between devices: 410 us -> 310 us  [send(): lax.ppermute(array, 'band', pairs(owners, shift))]
  transfers between devices with their start and end apart: 63 -> 63, of which waited for: 28 -> 25; matrix products, arithmetic and copies ran while one was open for 1% -> 1% of each run, Pallas kernels for 11% -> 11%
where the time goes in v2:
time: 858 us; the launch traced here: 852 us
  starting transfers between devices  399 us (47%)
  waiting for transfers between devices  310 us (36%)
  Pallas kernels  115 us (13%)
  between operations  14.5 us (2%)
  other arithmetic  8.83 us (1%)
    ppermute x62, starting transfers between devices, send(): lax.ppermute(array, 'band', pairs(owners, shift))  399 us
    ppermute x62, waiting for transfers between devices, send(): lax.ppermute(array, 'band', pairs(owners, shift))  310 us
    pallas_call x4, Pallas kernels, sums(): pl.pallas_call(functools.partial(sums_kernel, len(inputs), None if before...  78.1 us
    pallas_call x1, Pallas kernels, polar_sums(): pl.pallas_call(polar_kernel, out_shape=jax.ShapeDtypeStruct((blocks, widt...  21.8 us
  transfers between devices with their start and end apart: 63, of which 25 were waited for; matrix products, arithmetic and copies ran while one was open for 1% of the time, Pallas kernels for 11%

profile of v2, /device:TPU:69, one launch (start us, length us, event | category | flops | bytes accessed | tf_op | source)
XLA Modules:
  0.0 852.1 jit_solution(11200037482084855644)
XLA Ops:
  7.2 21.8 %polar.1 = f32[32,128,640]{2,1,0:T(8,128)} custom-call(s32[64]{0:T(128)} %slot_ref.1, s32[64]{0:T(128)} %place_ref.1, bf16[64,128,128]{2,1,0:T(8,128)(2,1)} %tiles_ref.9, bf16[64,128,640]{2,1,0:T(8,128)(2,1)} %bitcast.11), custom_call_target="tpu_custom_call" | custom-call | flops 1342177280 | bytes 20971520 | tf_op jit(solution)/shard_map/polar/pallas_call | solution.py:282
  31.9 13.3 %collective-permute-start.14 = (bf16[2,128,640]{2,1,0:T(8,128)(2,1)}, bf16[2,128,640]{2,1,0:T(8,128)(2,1)S(1)}, u32[]{:S(2)}, u32[]{:S(2)}) collective-permute-start(bf16[2,128,640]{2,1,0:T(8,128)(2,1)} %get-tuple-element.81), channel_id=1, source_target_pairs={{0,14},{1,15},{2,16},{3,17},{4,18},{5,19},{6,20},{7,21},{8,22},{9,... | collective-permute-start | bytes 983048 | tf_op jit(solution)/shard_map/ppermute | solution.py:305
  47.9 9.1 %pack.2 = (bf16[2,128,640]{2,1,0:T(8,128)(2,1)}, bf16[2,128,640]{2,1,0:T(8,128)(2,1)}, bf16[2,128,640]{2,1,0:T(8,128)(2,1)}, bf16[2,128,640]{2,1,0:T(8,128)(2,1)...) custom-call(s32[1]{0:T(128)} %bitcast.me_ref, ...), custom_call_target="tpu_custom_call" | custom-call | bytes 19660800 | tf_op jit(solution)/shard_map/pack/pallas_call | solution.py:96
  77.1 23.3 %collective-permute-start.7 = (bf16[2,128,640]{2,1,0:T(8,128)(2,1)}, bf16[2,128,640]{2,1,0:T(8,128)(2,1)S(1)}, u32[]{:S(2)}, u32[]{:S(2)}) collective-permute-start(bf16[2,128,640]{2,1,0:T(8,128)(2,1)} %get-tuple-element.73), channel_id=1, source_target_pairs={{0,22},{1,23},{2,24},{3,25},{4,26},{5,27},{6,28},{7,29},{8,30},{9,... | collective-permute-start | bytes 983048 | tf_op jit(solution)/shard_map/ppermute | solution.py:305
  100.6 14.5 %collective-permute-start.8 = (bf16[2,128,640]{2,1,0:T(8,128)(2,1)}, bf16[2,128,640]{2,1,0:T(8,128)(2,1)S(1)}, u32[]{:S(2)}, u32[]{:S(2)}) collective-permute-start(bf16[2,128,640]{2,1,0:T(8,128)(2,1)} %get-tuple-element.74), channel_id=1, source_target_pairs={{0,11},{1,10},{2,13},{3,12},{4,15},{5,14},{6,17},{7,16},{8,19},{9,... | collective-permute-start | bytes 983048 | tf_op jit(solution)/shard_map/ppermute | solution.py:305
  115.0 21.2 %collective-permute-done.4.refs_0_ = bf16[2,128,640]{2,1,0:T(8,128)(2,1)S(1)} collective-permute-done((bf16[2,128,640]{2,1,0:T(8,128)(2,1)}, bf16[2,128,640]{2,1,0:T(8,128)(2,1)S(1)}, u32[]{:S(2)}, u32[]{:S(2)}) %collective-permute-start.4) | collective-permute-done | bytes 327712 | tf_op jit(solution)/shard_map/ppermute | solution.py:305
  149.1 28.8 %collective-permute-done.6.refs_2_ = bf16[2,128,640]{2,1,0:T(8,128)(2,1)S(1)} collective-permute-done((bf16[2,128,640]{2,1,0:T(8,128)(2,1)}, bf16[2,128,640]{2,1,0:T(8,128)(2,1)S(1)}, u32[]{:S(2)}, u32[]{:S(2)}) %collective-permute-start.6) | collective-permute-done | bytes 327712 | tf_op jit(solution)/shard_map/ppermute | solution.py:305
  177.9 11.7 %collective-permute-start.12 = (bf16[2,128,640]{2,1,0:T(8,128)(2,1)}, bf16[2,128,640]{2,1,0:T(8,128)(2,1)S(1)}, u32[]{:S(2)}, u32[]{:S(2)}) collective-permute-start(bf16[2,128,640]{2,1,0:T(8,128)(2,1)} %get-tuple-element.78), channel_id=1, source_target_pairs={{0,13},{1,12},{2,15},{3,14},{4,17},{5,16},{6,19},{7,18},{8,21},{9,... | collective-permute-start | bytes 983048 | tf_op jit(solution)/shard_map/ppermute | solution.py:305
  189.7 26.7 %collective-permute-done.8.refs_4_ = bf16[2,128,640]{2,1,0:T(8,128)(2,1)S(1)} collective-permute-done((bf16[2,128,640]{2,1,0:T(8,128)(2,1)}, bf16[2,128,640]{2,1,0:T(8,128)(2,1)S(1)}, u32[]{:S(2)}, u32[]{:S(2)}) %collective-permute-start.8) | collective-permute-done | bytes 327712 | tf_op jit(solution)/shard_map/ppermute | solution.py:305
  222.1 34.9 %collective-permute-done.10.refs_6_ = bf16[2,128,640]{2,1,0:T(8,128)(2,1)S(1)} collective-permute-done((bf16[2,128,640]{2,1,0:T(8,128)(2,1)}, bf16[2,128,640]{2,1,0:T(8,128)(2,1)S(1)}, u32[]{:S(2)}, u32[]{:S(2)}) %collective-permute-start.10) | collective-permute-done | bytes 327712 | tf_op jit(solution)/shard_map/ppermute | solution.py:305
  263.4 32.9 %collective-permute-done.12.refs_8_ = bf16[2,128,640]{2,1,0:T(8,128)(2,1)S(1)} collective-permute-done((bf16[2,128,640]{2,1,0:T(8,128)(2,1)}, bf16[2,128,640]{2,1,0:T(8,128)(2,1)S(1)}, u32[]{:S(2)}, u32[]{:S(2)}) %collective-permute-start.12) | collective-permute-done | bytes 327712 | tf_op jit(solution)/shard_map/ppermute | solution.py:305
  313.0 8.9 %collective-permute-done.19.refs_6_ = bf16[2,128,640]{2,1,0:T(8,128)(2,1)S(1)} collective-permute-done((bf16[2,128,640]{2,1,0:T(8,128)(2,1)}, bf16[2,128,640]{2,1,0:T(8,128)(2,1)S(1)}, u32[]{:S(2)}, u32[]{:S(2)}) %collective-permute-start.19) | collective-permute-done | bytes 327712 | tf_op jit(solution)/shard_map/ppermute | solution.py:305
  326.0 9.5 %collective-permute-done.21.refs_8_ = bf16[2,128,640]{2,1,0:T(8,128)(2,1)S(1)} collective-permute-done((bf16[2,128,640]{2,1,0:T(8,128)(2,1)}, bf16[2,128,640]{2,1,0:T(8,128)(2,1)S(1)}, u32[]{:S(2)}, u32[]{:S(2)}) %collective-permute-start.21) | collective-permute-done | bytes 327712 | tf_op jit(solution)/shard_map/ppermute | solution.py:305
  345.4 9.2 %collective-permute-done.23.refs_10_ = bf16[2,128,640]{2,1,0:T(8,128)(2,1)S(1)} collective-permute-done((bf16[2,128,640]{2,1,0:T(8,128)(2,1)}, bf16[2,128,640]{2,1,0:T(8,128)(2,1)S(1)}, u32[]{:S(2)}, u32[]{:S(2)}) %collective-permute-start.23) | collective-permute-done | bytes 327712 | tf_op jit(solution)/shard_map/ppermute | solution.py:305
  362.3 18.7 %collective-permute-done.25.refs_12_ = bf16[2,128,640]{2,1,0:T(8,128)(2,1)S(1)} collective-permute-done((bf16[2,128,640]{2,1,0:T(8,128)(2,1)}, bf16[2,128,640]{2,1,0:T(8,128)(2,1)S(1)}, u32[]{:S(2)}, u32[]{:S(2)}) %collective-permute-start.25) | collective-permute-done | bytes 327712 | tf_op jit(solution)/shard_map/ppermute | solution.py:305
  383.1 12.1 %collective-permute-start.13 = (bf16[2,128,640]{2,1,0:T(8,128)(2,1)}, bf16[2,128,640]{2,1,0:T(8,128)(2,1)S(1)}, u32[]{:S(2)}, u32[]{:S(2)}) collective-permute-start(bf16[2,128,640]{2,1,0:T(8,128)(2,1)} %get-tuple-element.79), channel_id=1, source_target_pairs={{0,21},{1,20},{2,23},{3,22},{4,25},{5,24},{6,27},{7,26},{8,29},{9,... | collective-permute-start | bytes 983048 | tf_op jit(solution)/shard_map/ppermute | solution.py:305
  414.8 18.1 %collective-permute-done.29.refs_16_ = bf16[2,128,640]{2,1,0:T(8,128)(2,1)S(1)} collective-permute-done((bf16[2,128,640]{2,1,0:T(8,128)(2,1)}, bf16[2,128,640]{2,1,0:T(8,128)(2,1)S(1)}, u32[]{:S(2)}, u32[]{:S(2)}) %collective-permute-start.29) | collective-permute-done | bytes 327712 | tf_op jit(solution)/shard_map/ppermute | solution.py:305
  440.1 12.1 %collective-permute-start.3 = (bf16[2,128,640]{2,1,0:T(8,128)(2,1)}, bf16[2,128,640]{2,1,0:T(8,128)(2,1)S(1)}, u32[]{:S(2)}, u32[]{:S(2)}) collective-permute-start(bf16[2,128,640]{2,1,0:T(8,128)(2,1)} %get-tuple-element.69), channel_id=1, source_target_pairs={{0,17},{1,16},{2,19},{3,18},{4,21},{5,20},{6,23},{7,22},{8,25},{9,... | collective-permute-start | bytes 983048 | tf_op jit(solution)/shard_map/ppermute | solution.py:305
  452.3 34.6 %shard_map.131.refs_10_ = f32[32,128,640]{2,1,0:T(8,128)} custom-call(s32[2]{0:T(128)} %pad_add_fusion.2.bounds_ref, s32[256]{0:T(256)} %select_reduce_fusion.order_ref, s32[256]{0:T(256)} %get-tuple-element.136.slot_ref, s32[256]{0:T(256)} %copy-done.3, bf16[256,128,128]{2,1,0:T(8,128)(2,1)} %tiles_ref.8, bf16[2,128,640]{2,1,0:T(8,128)(2,1)} %get-tuple-element.80.refs_0_, ...), custom_call_target="tpu_custom_call" | custom-call | flops 3019898880 | bytes 15728640 | tf_op jit(solution)/shard_map/pallas_call | solution.py:190
  490.9 27.8 %shard_map.132.refs_4_ = f32[32,128,640]{2,1,0:T(8,128)} custom-call(s32[2]{0:T(128)S(1)} %pad_add_fusion.1.bounds_ref, s32[256]{0:T(256)S(1)} %copy-done.2, s32[256]{0:T(256)S(1)} %copy-done.1, s32[256]{0:T(256)S(1)} %copy-done.4, bf16[256,128,128]{2,1,0:T(8,128)(2,1)S(1)} %copy-done, bf16[2,128,640]{2,1,0:T(8,128)(2,1)S(1)} %collective-permute-done.4.refs_0_, ...), custom_call_target="tpu_custom_call" | custom-call | flops 1677721600 | bytes 15728640 | tf_op jit(solution)/shard_map/pallas_call | solution.py:190
  518.8 18.9 %collective-permute-done.1.refs_1_ = bf16[2,128,640]{2,1,0:T(8,128)(2,1)S(1)} collective-permute-done((bf16[2,128,640]{2,1,0:T(8,128)(2,1)}, bf16[2,128,640]{2,1,0:T(8,128)(2,1)S(1)}, u32[]{:S(2)}, u32[]{:S(2)}) %collective-permute-start.1) | collective-permute-done | bytes 327712 | tf_op jit(solution)/shard_map/ppermute | solution.py:305
  537.7 18.2 %collective-permute-done.3.refs_3_ = bf16[2,128,640]{2,1,0:T(8,128)(2,1)S(1)} collective-permute-done((bf16[2,128,640]{2,1,0:T(8,128)(2,1)}, bf16[2,128,640]{2,1,0:T(8,128)(2,1)S(1)}, u32[]{:S(2)}, u32[]{:S(2)}) %collective-permute-start.3) | collective-permute-done | bytes 327712 | tf_op jit(solution)/shard_map/ppermute | solution.py:305
  569.1 72.6 %collective-permute-start.33 = (bf16[128,640]{1,0:T(8,128)(2,1)S(1)}, bf16[128,640]{1,0:T(8,128)(2,1)S(1)}, u32[]{:S(2)}, u32[]{:S(2)}) collective-permute-start(bf16[128,640]{1,0:T(8,128)(2,1)S(1)} %get-tuple-element.101), channel_id=1, source_target_pairs={{0,19},{1,18},{2,21},{3,20},{4,23},{5,22},{6,25},{7,24},{8,27},{9,... | collective-permute-start | bytes 491528 | tf_op jit(solution)/shard_map/ppermute | solution.py:305
  641.8 9.1 %collective-permute-start.35 = (bf16[128,640]{1,0:T(8,128)(2,1)S(1)}, bf16[128,640]{1,0:T(8,128)(2,1)S(1)}, u32[]{:S(2)}, u32[]{:S(2)}) collective-permute-start(bf16[128,640]{1,0:T(8,128)(2,1)S(1)} %get-tuple-element.103), channel_id=1, source_target_pairs={{0,18},{1,19},{2,20},{3,21},{4,22},{5,23},{6,24},{7,25},{8,26},{9,... | collective-permute-start | bytes 491528 | tf_op jit(solution)/shard_map/ppermute | solution.py:305
  650.9 10.5 %shard_map.133 = (bf16[128,640]{1,0:T(8,128)(2,1)S(1)}, bf16[128,640]{1,0:T(8,128)(2,1)S(1)}, bf16[128,640]{1,0:T(8,128)(2,1)S(1)}, bf16[128,640]{1,0:T(8,128)(2...) custom-call(s32[2]{0:T(128)S(1)} %get-tuple-element.137.bounds_ref, ...), custom_call_target="tpu_custom_call" | custom-call | flops 503316480 | bytes 11796480 | tf_op jit(solution)/shard_map/pallas_call | solution.py:190
  661.4 29.6 %collective-permute-start.37 = (bf16[128,640]{1,0:T(8,128)(2,1)S(1)}, bf16[128,640]{1,0:T(8,128)(2,1)S(1)}, u32[]{:S(2)}, u32[]{:S(2)}) collective-permute-start(bf16[128,640]{1,0:T(8,128)(2,1)S(1)} %get-tuple-element.105), channel_id=1, source_target_pairs={{0,21},{1,20},{2,23},{3,22},{4,25},{5,24},{6,27},{7,26},{8,29},{9,... | collective-permute-start | bytes 491528 | tf_op jit(solution)/shard_map/ppermute | solution.py:305
  699.4 22.7 %collective-permute-start.41 = (bf16[128,640]{1,0:T(8,128)(2,1)S(1)}, bf16[128,640]{1,0:T(8,128)(2,1)S(1)}, u32[]{:S(2)}, u32[]{:S(2)}) collective-permute-start(bf16[128,640]{1,0:T(8,128)(2,1)S(1)} %get-tuple-element.109), channel_id=1, source_target_pairs={{0,23},{1,22},{2,25},{3,24},{4,27},{5,26},{6,29},{7,28},{8,31},{9,... | collective-permute-start | bytes 491528 | tf_op jit(solution)/shard_map/ppermute | solution.py:305
  743.1 11.3 %collective-permute-done.41.refs_11_ = bf16[128,640]{1,0:T(8,128)(2,1)S(1)} collective-permute-done((bf16[128,640]{1,0:T(8,128)(2,1)S(1)}, bf16[128,640]{1,0:T(8,128)(2,1)S(1)}, u32[]{:S(2)}, u32[]{:S(2)}) %collective-permute-start.41) | collective-permute-done | bytes 163872 | tf_op jit(solution)/shard_map/ppermute | solution.py:305
  754.4 9.6 %collective-permute-start.47 = (bf16[128,640]{1,0:T(8,128)(2,1)S(1)}, bf16[128,640]{1,0:T(8,128)(2,1)S(1)}, u32[]{:S(2)}, u32[]{:S(2)}) collective-permute-start(bf16[128,640]{1,0:T(8,128)(2,1)S(1)} %get-tuple-element.115), channel_id=1, source_target_pairs={{0,24},{1,25},{2,26},{3,27},{4,28},{5,29},{6,30},{7,31},{8,0},{9,1... | collective-permute-start | bytes 491528 | tf_op jit(solution)/shard_map/ppermute | solution.py:305
  770.5 9.9 %collective-permute-start.49 = (bf16[128,640]{1,0:T(8,128)(2,1)S(1)}, bf16[128,640]{1,0:T(8,128)(2,1)S(1)}, u32[]{:S(2)}, u32[]{:S(2)}) collective-permute-start(bf16[128,640]{1,0:T(8,128)(2,1)S(1)} %get-tuple-element.117), channel_id=1, source_target_pairs={{0,27},{1,26},{2,29},{3,28},{4,31},{5,30},{6,1},{7,0},{8,3},{9,2},... | collective-permute-start | bytes 491528 | tf_op jit(solution)/shard_map/ppermute | solution.py:305
  785.5 12.9 %collective-permute-start.51 = (bf16[128,640]{1,0:T(8,128)(2,1)S(1)}, bf16[128,640]{1,0:T(8,128)(2,1)S(1)}, u32[]{:S(2)}, u32[]{:S(2)}) collective-permute-start(bf16[128,640]{1,0:T(8,128)(2,1)S(1)} %get-tuple-element.119), channel_id=1, source_target_pairs={{0,26},{1,27},{2,28},{3,29},{4,30},{5,31},{6,0},{7,1},{8,2},{9,3},... | collective-permute-start | bytes 491528 | tf_op jit(solution)/shard_map/ppermute | solution.py:305
  798.4 13.2 %collective-permute-start.53 = (bf16[128,640]{1,0:T(8,128)(2,1)S(1)}, bf16[128,640]{1,0:T(8,128)(2,1)S(1)}, u32[]{:S(2)}, u32[]{:S(2)}) collective-permute-start(bf16[128,640]{1,0:T(8,128)(2,1)S(1)} %get-tuple-element.121), channel_id=1, source_target_pairs={{0,29},{1,28},{2,31},{3,30},{4,1},{5,0},{6,3},{7,2},{8,5},{9,4},{1... | collective-permute-start | bytes 491528 | tf_op jit(solution)/shard_map/ppermute | solution.py:305
  (176 shorter events, 210.1 us)
Async XLA Ops:
  7.2 836.4 %reduce-scatter.2.cloned.1.call-start = ((), (), s32[]{:S(2)}) async-start(), calls=%async_computation.1 | async-start | bytes 10813440 | tf_op jit(solution)/shard_map/reduce_scatter | solution.py:316
  45.3 55.3 %collective-permute-start.15 = (bf16[2,128,640]{2,1,0:T(8,128)(2,1)}, bf16[2,128,640]{2,1,0:T(8,128)(2,1)S(1)}, u32[]{:S(2)}, u32[]{:S(2)}) collective-permute-start(bf16[2,128,640]{2,1,0:T(8,128)(2,1)} %get-tuple-element.82), channel_id=1, source_target_pairs={{0,18},{1,19},{2,20},{3,21},{4,22},{5,23},{6,24},{7,25},{8,26},{9,... | collective-permute-start | bytes 983048 | tf_op jit(solution)/shard_map/ppermute | solution.py:305
  57.0 79.3 %collective-permute-start.4 = (bf16[2,128,640]{2,1,0:T(8,128)(2,1)}, bf16[2,128,640]{2,1,0:T(8,128)(2,1)S(1)}, u32[]{:S(2)}, u32[]{:S(2)}) collective-permute-start(bf16[2,128,640]{2,1,0:T(8,128)(2,1)} %get-tuple-element.70), channel_id=1, source_target_pairs={{0,9},{1,8},{2,11},{3,10},{4,13},{5,12},{6,15},{7,14},{8,17},{9,16... | collective-permute-start | bytes 983048 | tf_op jit(solution)/shard_map/ppermute | solution.py:305
  60.7 82.6 %collective-permute-start.5 = (bf16[2,128,640]{2,1,0:T(8,128)(2,1)}, bf16[2,128,640]{2,1,0:T(8,128)(2,1)S(1)}, u32[]{:S(2)}, u32[]{:S(2)}) collective-permute-start(bf16[2,128,640]{2,1,0:T(8,128)(2,1)} %get-tuple-element.71), channel_id=1, source_target_pairs={{0,25},{1,24},{2,27},{3,26},{4,29},{5,28},{6,31},{7,30},{8,1},{9,0... | collective-permute-start | bytes 983048 | tf_op jit(solution)/shard_map/ppermute | solution.py:305
  65.4 112.5 %collective-permute-start.6 = (bf16[2,128,640]{2,1,0:T(8,128)(2,1)}, bf16[2,128,640]{2,1,0:T(8,128)(2,1)S(1)}, u32[]{:S(2)}, u32[]{:S(2)}) collective-permute-start(bf16[2,128,640]{2,1,0:T(8,128)(2,1)} %get-tuple-element.72), channel_id=1, source_target_pairs={{0,10},{1,11},{2,12},{3,13},{4,14},{5,15},{6,16},{7,17},{8,18},{9,... | collective-permute-start | bytes 983048 | tf_op jit(solution)/shard_map/ppermute | solution.py:305
  77.1 100.7 %collective-permute-start.7 = (bf16[2,128,640]{2,1,0:T(8,128)(2,1)}, bf16[2,128,640]{2,1,0:T(8,128)(2,1)S(1)}, u32[]{:S(2)}, u32[]{:S(2)}) collective-permute-start(bf16[2,128,640]{2,1,0:T(8,128)(2,1)} %get-tuple-element.73), channel_id=1, source_target_pairs={{0,22},{1,23},{2,24},{3,25},{4,26},{5,27},{6,28},{7,29},{8,30},{9,... | collective-permute-start | bytes 983048 | tf_op jit(solution)/shard_map/ppermute | solution.py:305
  100.6 115.8 %collective-permute-start.8 = (bf16[2,128,640]{2,1,0:T(8,128)(2,1)}, bf16[2,128,640]{2,1,0:T(8,128)(2,1)S(1)}, u32[]{:S(2)}, u32[]{:S(2)}) collective-permute-start(bf16[2,128,640]{2,1,0:T(8,128)(2,1)} %get-tuple-element.74), channel_id=1, source_target_pairs={{0,11},{1,10},{2,13},{3,12},{4,15},{5,14},{6,17},{7,16},{8,19},{9,... | collective-permute-start | bytes 983048 | tf_op jit(solution)/shard_map/ppermute | solution.py:305
  136.2 81.0 %collective-permute-start.9 = (bf16[2,128,640]{2,1,0:T(8,128)(2,1)}, bf16[2,128,640]{2,1,0:T(8,128)(2,1)S(1)}, u32[]{:S(2)}, u32[]{:S(2)}) collective-permute-start(bf16[2,128,640]{2,1,0:T(8,128)(2,1)} %get-tuple-element.75), channel_id=1, source_target_pairs={{0,23},{1,22},{2,25},{3,24},{4,27},{5,26},{6,29},{7,28},{8,31},{9,... | collective-permute-start | bytes 983048 | tf_op jit(solution)/shard_map/ppermute | solution.py:305
  143.4 113.6 %collective-permute-start.10 = (bf16[2,128,640]{2,1,0:T(8,128)(2,1)}, bf16[2,128,640]{2,1,0:T(8,128)(2,1)S(1)}, u32[]{:S(2)}, u32[]{:S(2)}) collective-permute-start(bf16[2,128,640]{2,1,0:T(8,128)(2,1)} %get-tuple-element.76), channel_id=1, source_target_pairs={{0,12},{1,13},{2,14},{3,15},{4,16},{5,17},{6,18},{7,19},{8,20},{9,... | collective-permute-start | bytes 983048 | tf_op jit(solution)/shard_map/ppermute | solution.py:305
  177.9 79.1 %collective-permute-start.11 = (bf16[2,128,640]{2,1,0:T(8,128)(2,1)}, bf16[2,128,640]{2,1,0:T(8,128)(2,1)S(1)}, u32[]{:S(2)}, u32[]{:S(2)}) collective-permute-start(bf16[2,128,640]{2,1,0:T(8,128)(2,1)} %get-tuple-element.77), channel_id=1, source_target_pairs={{0,20},{1,21},{2,22},{3,23},{4,24},{5,25},{6,26},{7,27},{8,28},{9,... | collective-permute-start | bytes 983048 | tf_op jit(solution)/shard_map/ppermute | solution.py:305
  177.9 118.5 %collective-permute-start.12 = (bf16[2,128,640]{2,1,0:T(8,128)(2,1)}, bf16[2,128,640]{2,1,0:T(8,128)(2,1)S(1)}, u32[]{:S(2)}, u32[]{:S(2)}) collective-permute-start(bf16[2,128,640]{2,1,0:T(8,128)(2,1)} %get-tuple-element.78), channel_id=1, source_target_pairs={{0,13},{1,12},{2,15},{3,14},{4,17},{5,16},{6,19},{7,18},{8,21},{9,... | collective-permute-start | bytes 983048 | tf_op jit(solution)/shard_map/ppermute | solution.py:305
  216.3 82.4 %collective-permute-start.16 = (bf16[2,128,640]{2,1,0:T(8,128)(2,1)}, bf16[2,128,640]{2,1,0:T(8,128)(2,1)S(1)}, u32[]{:S(2)}, u32[]{:S(2)}) collective-permute-start(bf16[2,128,640]{2,1,0:T(8,128)(2,1)} %get-tuple-element.83), channel_id=1, source_target_pairs={{0,1},{1,0},{2,3},{3,2},{4,5},{5,4},{6,7},{7,6},{8,9},{9,8},{10,11... | collective-permute-start | bytes 983048 | tf_op jit(solution)/shard_map/ppermute | solution.py:305
  217.3 92.5 %collective-permute-start.17 = (bf16[2,128,640]{2,1,0:T(8,128)(2,1)}, bf16[2,128,640]{2,1,0:T(8,128)(2,1)S(1)}, u32[]{:S(2)}, u32[]{:S(2)}) collective-permute-start(bf16[2,128,640]{2,1,0:T(8,128)(2,1)} %get-tuple-element.84), channel_id=1, source_target_pairs={{0,2},{1,3},{2,4},{3,5},{4,6},{5,7},{6,8},{7,9},{8,10},{9,11},{10,... | collective-permute-start | bytes 983048 | tf_op jit(solution)/shard_map/ppermute | solution.py:305
  257.0 52.9 %collective-permute-start.18 = (bf16[2,128,640]{2,1,0:T(8,128)(2,1)}, bf16[2,128,640]{2,1,0:T(8,128)(2,1)S(1)}, u32[]{:S(2)}, u32[]{:S(2)}) collective-permute-start(bf16[2,128,640]{2,1,0:T(8,128)(2,1)} %get-tuple-element.85), channel_id=1, source_target_pairs={{0,30},{1,31},{2,0},{3,1},{4,2},{5,3},{6,4},{7,5},{8,6},{9,7},{10,... | collective-permute-start | bytes 983048 | tf_op jit(solution)/shard_map/ppermute | solution.py:305
  257.0 64.9 %collective-permute-start.19 = (bf16[2,128,640]{2,1,0:T(8,128)(2,1)}, bf16[2,128,640]{2,1,0:T(8,128)(2,1)S(1)}, u32[]{:S(2)}, u32[]{:S(2)}) collective-permute-start(bf16[2,128,640]{2,1,0:T(8,128)(2,1)} %get-tuple-element.86), channel_id=1, source_target_pairs={{0,3},{1,2},{2,5},{3,4},{4,7},{5,6},{6,9},{7,8},{8,11},{9,10},{10,... | collective-permute-start | bytes 983048 | tf_op jit(solution)/shard_map/ppermute | solution.py:305
  321.9 59.1 %collective-permute-start.25 = (bf16[2,128,640]{2,1,0:T(8,128)(2,1)}, bf16[2,128,640]{2,1,0:T(8,128)(2,1)S(1)}, u32[]{:S(2)}, u32[]{:S(2)}) collective-permute-start(bf16[2,128,640]{2,1,0:T(8,128)(2,1)} %get-tuple-element.92), channel_id=1, source_target_pairs={{0,6},{1,7},{2,8},{3,9},{4,10},{5,11},{6,12},{7,13},{8,14},{9,15},... | collective-permute-start | bytes 983048 | tf_op jit(solution)/shard_map/ppermute | solution.py:305
  339.1 65.8 %collective-permute-start.27 = (bf16[2,128,640]{2,1,0:T(8,128)(2,1)}, bf16[2,128,640]{2,1,0:T(8,128)(2,1)S(1)}, u32[]{:S(2)}, u32[]{:S(2)}) collective-permute-start(bf16[2,128,640]{2,1,0:T(8,128)(2,1)} %get-tuple-element.94), channel_id=1, source_target_pairs={{0,7},{1,6},{2,9},{3,8},{4,11},{5,10},{6,13},{7,12},{8,15},{9,14},... | collective-permute-start | bytes 983048 | tf_op jit(solution)/shard_map/ppermute | solution.py:305
  354.5 56.8 %collective-permute-start.28 = (bf16[2,128,640]{2,1,0:T(8,128)(2,1)}, bf16[2,128,640]{2,1,0:T(8,128)(2,1)S(1)}, u32[]{:S(2)}, u32[]{:S(2)}) collective-permute-start(bf16[2,128,640]{2,1,0:T(8,128)(2,1)} %get-tuple-element.95), channel_id=1, source_target_pairs={{0,27},{1,26},{2,29},{3,28},{4,31},{5,30},{6,1},{7,0},{8,3},{9,2},... | collective-permute-start | bytes 983048 | tf_op jit(solution)/shard_map/ppermute | solution.py:305
  357.1 75.8 %collective-permute-start.29 = (bf16[2,128,640]{2,1,0:T(8,128)(2,1)}, bf16[2,128,640]{2,1,0:T(8,128)(2,1)S(1)}, u32[]{:S(2)}, u32[]{:S(2)}) collective-permute-start(bf16[2,128,640]{2,1,0:T(8,128)(2,1)} %get-tuple-element.96), channel_id=1, source_target_pairs={{0,8},{1,9},{2,10},{3,11},{4,12},{5,13},{6,14},{7,15},{8,16},{9,17... | collective-permute-start | bytes 983048 | tf_op jit(solution)/shard_map/ppermute | solution.py:305
  381.0 59.1 %collective-permute-start.30 = (bf16[2,128,640]{2,1,0:T(8,128)(2,1)}, bf16[2,128,640]{2,1,0:T(8,128)(2,1)S(1)}, u32[]{:S(2)}, u32[]{:S(2)}) collective-permute-start(bf16[2,128,640]{2,1,0:T(8,128)(2,1)} %get-tuple-element.97), channel_id=1, source_target_pairs={{0,24},{1,25},{2,26},{3,27},{4,28},{5,29},{6,30},{7,31},{8,0},{9,1... | collective-permute-start | bytes 983048 | tf_op jit(solution)/shard_map/ppermute | solution.py:305
  383.1 103.8 %collective-permute-start.13 = (bf16[2,128,640]{2,1,0:T(8,128)(2,1)}, bf16[2,128,640]{2,1,0:T(8,128)(2,1)S(1)}, u32[]{:S(2)}, u32[]{:S(2)}) collective-permute-start(bf16[2,128,640]{2,1,0:T(8,128)(2,1)} %get-tuple-element.79), channel_id=1, source_target_pairs={{0,21},{1,20},{2,23},{3,22},{4,25},{5,24},{6,27},{7,26},{8,29},{9,... | collective-permute-start | bytes 983048 | tf_op jit(solution)/shard_map/ppermute | solution.py:305
  404.9 113.9 %collective-permute-start = (bf16[2,128,640]{2,1,0:T(8,128)(2,1)}, bf16[2,128,640]{2,1,0:T(8,128)(2,1)S(1)}, u32[]{:S(2)}, u32[]{:S(2)}) collective-permute-start(bf16[2,128,640]{2,1,0:T(8,128)(2,1)} %get-tuple-element.66), channel_id=1, source_target_pairs={{0,15},{1,14},{2,17},{3,16},{4,19},{5,18},{6,21},{7,20},{8,23},{9,... | collective-permute-start | bytes 983048 | tf_op jit(solution)/shard_map/ppermute | solution.py:305
  411.4 126.3 %collective-permute-start.1 = (bf16[2,128,640]{2,1,0:T(8,128)(2,1)}, bf16[2,128,640]{2,1,0:T(8,128)(2,1)S(1)}, u32[]{:S(2)}, u32[]{:S(2)}) collective-permute-start(bf16[2,128,640]{2,1,0:T(8,128)(2,1)} %get-tuple-element.67), channel_id=1, source_target_pairs={{0,19},{1,18},{2,21},{3,20},{4,23},{5,22},{6,25},{7,24},{8,27},{9,... | collective-permute-start | bytes 983048 | tf_op jit(solution)/shard_map/ppermute | solution.py:305
  432.9 104.8 %collective-permute-start.2 = (bf16[2,128,640]{2,1,0:T(8,128)(2,1)}, bf16[2,128,640]{2,1,0:T(8,128)(2,1)S(1)}, u32[]{:S(2)}, u32[]{:S(2)}) collective-permute-start(bf16[2,128,640]{2,1,0:T(8,128)(2,1)} %get-tuple-element.68), channel_id=1, source_target_pairs={{0,16},{1,17},{2,18},{3,19},{4,20},{5,21},{6,22},{7,23},{8,24},{9,... | collective-permute-start | bytes 983048 | tf_op jit(solution)/shard_map/ppermute | solution.py:305
  440.1 115.7 %collective-permute-start.3 = (bf16[2,128,640]{2,1,0:T(8,128)(2,1)}, bf16[2,128,640]{2,1,0:T(8,128)(2,1)S(1)}, u32[]{:S(2)}, u32[]{:S(2)}) collective-permute-start(bf16[2,128,640]{2,1,0:T(8,128)(2,1)} %get-tuple-element.69), channel_id=1, source_target_pairs={{0,17},{1,16},{2,19},{3,18},{4,21},{5,20},{6,23},{7,22},{8,25},{9,... | collective-permute-start | bytes 983048 | tf_op jit(solution)/shard_map/ppermute | solution.py:305
  561.1 89.8 %collective-permute-start.31 = (bf16[128,640]{1,0:T(8,128)(2,1)S(1)}, bf16[128,640]{1,0:T(8,128)(2,1)S(1)}, u32[]{:S(2)}, u32[]{:S(2)}) collective-permute-start(bf16[128,640]{1,0:T(8,128)(2,1)S(1)} %get-tuple-element.99), channel_id=1, source_target_pairs={{0,17},{1,16},{2,19},{3,18},{4,21},{5,20},{6,23},{7,22},{8,25},{9,... | collective-permute-start | bytes 491528 | tf_op jit(solution)/shard_map/ppermute | solution.py:305
  564.6 96.8 %collective-permute-start.32 = (bf16[128,640]{1,0:T(8,128)(2,1)S(1)}, bf16[128,640]{1,0:T(8,128)(2,1)S(1)}, u32[]{:S(2)}, u32[]{:S(2)}) collective-permute-start(bf16[128,640]{1,0:T(8,128)(2,1)S(1)} %get-tuple-element.100), channel_id=1, source_target_pairs={{0,16},{1,17},{2,18},{3,19},{4,20},{5,21},{6,22},{7,23},{8,24},{9,... | collective-permute-start | bytes 491528 | tf_op jit(solution)/shard_map/ppermute | solution.py:305
  569.1 121.9 %collective-permute-start.33 = (bf16[128,640]{1,0:T(8,128)(2,1)S(1)}, bf16[128,640]{1,0:T(8,128)(2,1)S(1)}, u32[]{:S(2)}, u32[]{:S(2)}) collective-permute-start(bf16[128,640]{1,0:T(8,128)(2,1)S(1)} %get-tuple-element.101), channel_id=1, source_target_pairs={{0,19},{1,18},{2,21},{3,20},{4,23},{5,22},{6,25},{7,24},{8,27},{9,... | collective-permute-start | bytes 491528 | tf_op jit(solution)/shard_map/ppermute | solution.py:305
  641.8 49.3 %collective-permute-start.34 = (bf16[128,640]{1,0:T(8,128)(2,1)S(1)}, bf16[128,640]{1,0:T(8,128)(2,1)S(1)}, u32[]{:S(2)}, u32[]{:S(2)}) collective-permute-start(bf16[128,640]{1,0:T(8,128)(2,1)S(1)} %get-tuple-element.102), channel_id=1, source_target_pairs={{0,15},{1,14},{2,17},{3,16},{4,19},{5,18},{6,21},{7,20},{8,23},{9,... | collective-permute-start | bytes 491528 | tf_op jit(solution)/shard_map/ppermute | solution.py:305
  641.8 57.7 %collective-permute-start.35 = (bf16[128,640]{1,0:T(8,128)(2,1)S(1)}, bf16[128,640]{1,0:T(8,128)(2,1)S(1)}, u32[]{:S(2)}, u32[]{:S(2)}) collective-permute-start(bf16[128,640]{1,0:T(8,128)(2,1)S(1)} %get-tuple-element.103), channel_id=1, source_target_pairs={{0,18},{1,19},{2,20},{3,21},{4,22},{5,23},{6,24},{7,25},{8,26},{9,... | collective-permute-start | bytes 491528 | tf_op jit(solution)/shard_map/ppermute | solution.py:305
  661.4 60.7 %collective-permute-start.37 = (bf16[128,640]{1,0:T(8,128)(2,1)S(1)}, bf16[128,640]{1,0:T(8,128)(2,1)S(1)}, u32[]{:S(2)}, u32[]{:S(2)}) collective-permute-start(bf16[128,640]{1,0:T(8,128)(2,1)S(1)} %get-tuple-element.105), channel_id=1, source_target_pairs={{0,21},{1,20},{2,23},{3,22},{4,25},{5,24},{6,27},{7,26},{8,29},{9,... | collective-permute-start | bytes 491528 | tf_op jit(solution)/shard_map/ppermute | solution.py:305
  699.4 55.0 %collective-permute-start.41 = (bf16[128,640]{1,0:T(8,128)(2,1)S(1)}, bf16[128,640]{1,0:T(8,128)(2,1)S(1)}, u32[]{:S(2)}, u32[]{:S(2)}) collective-permute-start(bf16[128,640]{1,0:T(8,128)(2,1)S(1)} %get-tuple-element.109), channel_id=1, source_target_pairs={{0,23},{1,22},{2,25},{3,24},{4,27},{5,26},{6,29},{7,28},{8,31},{9,... | collective-permute-start | bytes 491528 | tf_op jit(solution)/shard_map/ppermute | solution.py:305
  (60 other events, 4198.3 us)
Sparse Core Ops, SparseCore 0:
  29.3 551.8 reduce-scatter.1
